TPU v7x, 8 devices: a whole 2x2x1 slice. The times are simulated.
8 devices in a mesh: dp: 2 (over z, y), ws: 4 (over x, core).
Axes of the slice: x: 2, y: 2, z: 1, core: 2. Of those that a mesh axis runs over, the one named last changes fastest.
Arguments:
- hidden: bfloat16 [128, 768], P(('dp', 'ws')), parts along dimension 0
- self_k: bfloat16 [128, 12, 384, 64], P(('dp', 'ws')), parts along dimension 0
- self_v: bfloat16 [128, 12, 384, 64], P(('dp', 'ws')), parts along dimension 0
- cross_k: bfloat16 [128, 12, 1024, 64], P(('dp', 'ws')), parts along dimension 0
- cross_v: bfloat16 [128, 12, 1024, 64], P(('dp', 'ws')), parts along dimension 0
- positions: int32 [128], P(('dp', 'ws')), parts along dimension 0
- enc_mask: int32 [128, 1024], P(('dp', 'ws')), parts along dimension 0
- rel_bias: float32 [12, 384], replicated
- expert_idx: int32 [128], P(('dp', 'ws')), parts along dimension 0
- ln_self: float32 [768], replicated
- ln_cross: float32 [768], replicated
- ln_ffn: float32 [768], replicated
- wq_self: bfloat16 [768, 768], P(None, 'ws')
- wk_self: bfloat16 [768, 768], P(None, 'ws')
- wv_self: bfloat16 [768, 768], P(None, 'ws')
- wo_self: bfloat16 [768, 768], P(None, 'ws')
- wq_cross: bfloat16 [768, 768], P(None, 'ws')
- wo_cross: bfloat16 [768, 768], P(None, 'ws')
- w_router: float32 [768, 16], P(None, 'ws')
- w_in: bfloat16 [16, 768, 3072], P(None, None, 'ws')
- w_out: bfloat16 [16, 3072, 768], P(None, 'ws')
Outputs:
- output 1: bfloat16 [128, 768], P(('dp', 'ws')), parts along dimension 0
- output 2: bfloat16 [128, 12, 384, 64], P(('dp', 'ws')), parts along dimension 0
- output 3: bfloat16 [128, 12, 384, 64], P(('dp', 'ws')), parts along dimension 0
There are 2 independent parts. A program takes and returns all parts, laid end to end along the dimension named above; an argument that names none is the same for every part.
All inputs are finite; a program needn't handle non-finite values.
Results may differ from a plain program's by a relative error of at most 0.0108291.
Values are sent between devices in bfloat16 or wider.
A program may use at most 1 GiB of HBM per device.

v0:
```python
import functools
import jax
import jax.numpy as jnp
from jax import lax
from jax.sharding import PartitionSpec as P

EPSILON = 1e-6
NEG_BIG = -1e30


def rms_norm(hidden, scale):
    hid_f32 = hidden.astype(jnp.float32)
    inv_rms = lax.rsqrt(jnp.mean(hid_f32 * hid_f32, axis=-1, keepdims=True) + EPSILON)
    return (hid_f32 * inv_rms * scale).astype(jnp.bfloat16)


def project(x_norm, weight):
    return jnp.dot(x_norm, weight, preferred_element_type=jnp.float32).astype(jnp.bfloat16)


def attend(queries, cache_keys, cache_vals, score_bias):
    scores = jnp.einsum('bhd,bhld->bhl', queries, cache_keys, preferred_element_type=jnp.float32) + score_bias
    attn_probs = jax.nn.softmax(scores, axis=-1).astype(jnp.bfloat16)
    context = jnp.einsum('bhl,bhld->bhd', attn_probs, cache_vals, preferred_element_type=jnp.float32)
    return context.astype(jnp.bfloat16)


def self_bias(rel_bias, positions, cache_len):
    distance = positions[:, None] - jnp.arange(cache_len)[None, :]
    pos_bias = jnp.take(rel_bias, jnp.clip(distance, 0, cache_len - 1), axis=1)
    pos_bias = jnp.where(distance[None] >= 0, pos_bias, NEG_BIG).transpose(1, 0, 2)
    return distance, pos_bias


def solution(mesh):
    ws_size = mesh.shape['ws']
    row_axes = ('dp', 'ws')
    row_vec = P(row_axes)
    row_mat = P(row_axes, None)
    cache_spec = P(row_axes, None, None, None)
    col_split = P(None, 'ws')
    in_specs = (row_mat, cache_spec, cache_spec, cache_spec, cache_spec, row_vec, row_mat, P(None, None), row_vec,
                P(None), P(None), P(None), col_split, col_split, col_split, col_split, col_split, col_split,
                col_split, P(None, None, 'ws'), P(None, 'ws', None))
    out_specs = (row_mat, cache_spec, cache_spec)

    def decoder_block(hidden, self_k, self_v, cross_k, cross_v, positions, enc_mask, rel_bias, expert_idx,
                      ln_self, ln_cross, ln_ffn, wq_self, wk_self, wv_self, wo_self, wq_cross, wo_cross,
                      w_router, w_in, w_out):
        gather_ws = functools.partial(lax.all_gather, axis_name='ws', tiled=True)
        wq_full = gather_ws(wq_self, axis=1)
        wk_full = gather_ws(wk_self, axis=1)
        wv_full = gather_ws(wv_self, axis=1)
        wo_full = gather_ws(wo_self, axis=1)
        wqc_full = gather_ws(wq_cross, axis=1)
        woc_full = gather_ws(wo_cross, axis=1)
        router_full = gather_ws(w_router, axis=1)
        win_full = gather_ws(w_in, axis=2)
        wout_full = gather_ws(w_out, axis=1)
        idx_all = gather_ws(expert_idx, axis=0)

        local_rows = hidden.shape[0]
        num_heads = rel_bias.shape[0]
        head_shape = (local_rows, num_heads, wq_full.shape[1] // num_heads)
        experts = win_full.shape[0]
        group_rows = local_rows * ws_size
        capacity = (2 * group_rows + experts - 1) // experts

        x_norm = rms_norm(hidden, ln_self)
        queries = project(x_norm, wq_full).reshape(head_shape)
        k_new = project(x_norm, wk_full).reshape(head_shape)
        v_new = project(x_norm, wv_full).reshape(head_shape)
        distance, pos_bias = self_bias(rel_bias, positions, self_k.shape[2])
        write_mask = (distance == 0)[:, None, :, None]
        new_self_k = jnp.where(write_mask, k_new[:, :, None, :], self_k)
        new_self_v = jnp.where(write_mask, v_new[:, :, None, :], self_v)
        context = attend(queries, new_self_k, new_self_v, pos_bias).reshape(local_rows, -1)
        after_self = (hidden.astype(jnp.float32) + jnp.dot(context, wo_full, preferred_element_type=jnp.float32)).astype(jnp.bfloat16)

        x_norm = rms_norm(after_self, ln_cross)
        queries = project(x_norm, wqc_full).reshape(head_shape)
        mask_bias = jnp.where(enc_mask == 1, 0.0, NEG_BIG)[:, None, :]
        context = attend(queries, cross_k, cross_v, mask_bias).reshape(local_rows, -1)
        after_cross = (after_self.astype(jnp.float32) + jnp.dot(context, woc_full, preferred_element_type=jnp.float32)).astype(jnp.bfloat16)

        x_norm = rms_norm(after_cross, ln_ffn)
        logits = jnp.dot(x_norm.astype(jnp.float32), router_full, precision=lax.Precision.HIGHEST,
                         preferred_element_type=jnp.float32)
        router_probs = jax.nn.softmax(logits, axis=-1)
        chosen = jnp.arange(experts)[None, :] == expert_idx[:, None]
        gate_val = jnp.sum(jnp.where(chosen, router_probs, 0.0), axis=-1)
        row_ids = lax.axis_index('ws') * local_rows + jnp.arange(local_rows)
        earlier = (idx_all[None, :] == expert_idx[:, None]) & (jnp.arange(group_rows)[None, :] < row_ids[:, None])
        slot_idx = jnp.sum(earlier.astype(jnp.int32), axis=1)
        keep_gate = jnp.where(slot_idx < capacity, gate_val, 0.0)
        ffn_hidden = jnp.einsum('bd,bdf->bf', x_norm, jnp.take(win_full, expert_idx, axis=0),
                                preferred_element_type=jnp.float32)
        ffn_hidden = jax.nn.relu(ffn_hidden).astype(jnp.bfloat16)
        expert_out = jnp.einsum('bf,bfd->bd', ffn_hidden, jnp.take(wout_full, expert_idx, axis=0),
                                preferred_element_type=jnp.float32).astype(jnp.bfloat16)
        hidden_out = (after_cross.astype(jnp.float32) + expert_out.astype(jnp.float32) * keep_gate[:, None]).astype(jnp.bfloat16)
        return hidden_out, new_self_k, new_self_v

    return jax.shard_map(decoder_block, mesh=mesh, in_specs=in_specs, out_specs=out_specs, check_vma=False)
```

profile of v0, /device:TPU:0, one launch (start us, length us, event | category | flops | bytes accessed | tf_op | source)
XLA Modules:
  0.0 1124.4 jit_solution(12717497960984666473)
XLA Ops:
  13.0 10.4 all-gather
  23.5 21.0 %gather_fusion = f32[6144,12]{1,0:T(8,128)} fusion(f32[12,384]{0,1:T(8,128)S(1)} %copy.27, s32[6144]{0:T(1024)S(1)} %broadcast_clamp_fusion), kind=kCustom, calls=%fused_computation | custom fusion | bytes 614400 | tf_op jit(solution)/shard_map/jit(_take)/gather | solution.py:30
  46.0 4.3 all-reduce
  55.1 4.3 all-gather.10.cloned.1.call-done
  61.2 12.2 %broadcast_select_fusion = (bf16[16,12,384,64]{2,3,1,0:T(8,128)(2,1)}, bf16[16,12,384,64]{2,3,1,0:T(8,128)(2,1)S(1)}) fusion(bf16[16,12,384,64]{2,3,1,0:T(8,128)(2,1)} %param.23, pred[16,384]{1,0:T(8,128)(4,1)S(1)} %get-tuple-element.13, bf16[16,12,64]{2,1,0:T(8,128)(2,1)S(1)} %broadcast_in_dim.119, bf16[16,12,384,64]{2,3,1,0:T(8,128)(2,1)} %param.22, ...), kind=kLoop, calls=%fused_computation.27 | loop fusion | flops 9437184 | bytes 37804032 | tf_op jit(solution)/shard_map/jit(_where)/select_n | solution.py:76
  73.4 3.7 copy-done
  80.0 5.1 fusion.18
  85.1 2.3 copy.30
  87.4 7.0 fusion.69
  98.3 9.9 fusion.70
  109.2 11.6 %fusion.29 = bf16[16,12,1,64]{3,2,1,0:T(2,128)(2,1)S(1)} fusion(bf16[16,12,1024,64]{2,3,1,0:T(8,128)(2,1)} %param.25, bf16[16,12,1024,1]{2,0,1,3:T(8,128)(2,1)S(1)} %fusion.23), kind=kOutput, calls=%fused_computation.50 | convolution fusion | flops 25165824 | bytes 25583616 | tf_op jit(solution)/shard_map/bhl,bhld->bhd/dot_general | solution.py:24
  121.0 1.8 multiply_reduce_fusion
  123.7 423.2 %all-gather.22.cloned.1.call-done = bf16[16,768,3072]{2,1,0:T(8,128)(2,1)} async-done(((bf16[16,768,768]{2,1,0:T(8,128)(2,1)}), bf16[16,768,3072]{2,1,0:T(8,128)(2,1)}) %all-gather.22.cloned.1.call-update) | async-done | bytes 75497488 | tf_op jit(solution)/shard_map/all_gather | solution.py:58
  546.9 48.6 %fusion.65 = (bf16[16,768,1024]{2,1,0:T(8,128)(2,1)}, bf16[16,768,1024]{2,1,0:T(8,128)(2,1)}, bf16[16,768,1024]{2,1,0:T(8,128)(2,1)}) fusion(bf16[16,768,3072]{2,1,0:T(8,128)(2,1)} %all-gather.22.cloned.1.call-done), kind=kLoop, calls=%fused_computation.110 | loop fusion | bytes 150994944 | tf_op jit(solution)/shard_map/jit(_take)/gather | solution.py:96
  595.5 18.6 %gather_fusion.1 = bf16[16,768,1024]{2,1,0:T(8,128)(2,1)} fusion(bf16[16,768,1024]{2,1,0:T(8,128)(2,1)} %get-tuple-element.3, s32[1024]{0:T(1024)S(1)} %pad_clamp_fusion), kind=kCustom, calls=%fused_computation.1 | custom fusion | bytes 50331712 | tf_op jit(solution)/shard_map/jit(_take)/gather | solution.py:96
  614.1 18.3 %gather_fusion.2 = bf16[16,768,1024]{2,1,0:T(8,128)(2,1)} fusion(bf16[16,768,1024]{2,1,0:T(8,128)(2,1)} %get-tuple-element.4, s32[1024]{0:T(1024)S(1)} %pad_clamp_fusion), kind=kCustom, calls=%fused_computation.2 | custom fusion | bytes 50331712 | tf_op jit(solution)/shard_map/jit(_take)/gather | solution.py:96
  632.4 18.3 %gather_fusion.3 = bf16[16,768,1024]{2,1,0:T(8,128)(2,1)} fusion(bf16[16,768,1024]{2,1,0:T(8,128)(2,1)} %get-tuple-element.5, s32[1024]{0:T(1024)S(1)} %pad_clamp_fusion), kind=kCustom, calls=%fused_computation.3 | custom fusion | bytes 50331712 | tf_op jit(solution)/shard_map/jit(_take)/gather | solution.py:96
  650.7 27.4 %fusion.4 = bf16[16,1,3072]{2,1,0:T(2,128)(2,1)S(1)} fusion(bf16[16,768,1024]{2,1,0:T(8,128)(2,1)} %gather_fusion.3, bf16[16,768,1024]{2,1,0:T(8,128)(2,1)} %gather_fusion.2, bf16[16,768,1024]{2,1,0:T(8,128)(2,1)} %gather_fusion.1, pred[16]{0:T(512)(128)(4,1)S(1)} %compare_and_fusion, bf16[16,768,1]{1,0,2:T(8,128)(2,1)S(1)} %fusion.61), kind=kOutput, calls=%fused_computation.12 | convolution fusion | flops 339738624 | bytes 75620368 | tf_op jit(solution)/shard_map/bd,bdf->bf/dot_general | solution.py:96
  678.1 308.9 %all-gather.24.cloned.1.call-done = bf16[16,3072,768]{2,1,0:T(8,128)(2,1)} async-done(((bf16[16,768,768]{2,1,0:T(8,128)(2,1)}), bf16[16,3072,768]{2,1,0:T(8,128)(2,1)}) %all-gather.24.cloned.1.call-update) | async-done | bytes 75497488 | tf_op jit(solution)/shard_map/all_gather | solution.py:59
  987.0 49.5 %fusion.66 = (bf16[16,1024,768]{2,1,0:T(8,128)(2,1)}, bf16[16,1024,768]{2,1,0:T(8,128)(2,1)}, bf16[16,1024,768]{2,1,0:T(8,128)(2,1)}) fusion(bf16[16,3072,768]{2,1,0:T(8,128)(2,1)} %all-gather.24.cloned.1.call-done), kind=kLoop, calls=%fused_computation.111 | loop fusion | bytes 150994944 | tf_op jit(solution)/shard_map/jit(_take)/gather | solution.py:99
  1036.5 18.2 %gather_fusion.4 = bf16[16,1024,768]{2,1,0:T(8,128)(2,1)} fusion(bf16[16,1024,768]{2,1,0:T(8,128)(2,1)} %get-tuple-element.6, s32[1024]{0:T(1024)S(1)} %pad_clamp_fusion), kind=kCustom, calls=%fused_computation.4 | custom fusion | bytes 50331712 | tf_op jit(solution)/shard_map/jit(_take)/gather | solution.py:99
  1054.8 18.2 %gather_fusion.5 = bf16[16,1024,768]{2,1,0:T(8,128)(2,1)} fusion(bf16[16,1024,768]{2,1,0:T(8,128)(2,1)} %get-tuple-element.7, s32[1024]{0:T(1024)S(1)} %pad_clamp_fusion), kind=kCustom, calls=%fused_computation.5 | custom fusion | bytes 50331712 | tf_op jit(solution)/shard_map/jit(_take)/gather | solution.py:99
  1073.0 18.2 %gather_fusion.6 = bf16[16,1024,768]{2,1,0:T(8,128)(2,1)} fusion(bf16[16,1024,768]{2,1,0:T(8,128)(2,1)} %get-tuple-element.8, s32[1024]{0:T(1024)S(1)} %pad_clamp_fusion), kind=kCustom, calls=%fused_computation.6 | custom fusion | bytes 50331712 | tf_op jit(solution)/shard_map/jit(_take)/gather | solution.py:99
  1091.3 25.6 %fusion.9 = bf16[16,1,768]{2,1,0:T(2,128)(2,1)S(1)} fusion(bf16[16,1024,768]{2,1,0:T(8,128)(2,1)} %gather_fusion.6, bf16[16,1024,768]{2,1,0:T(8,128)(2,1)} %gather_fusion.5, bf16[16,1024,768]{2,1,0:T(8,128)(2,1)} %gather_fusion.4, pred[16]{0:T(512)(128)(4,1)S(1)} %compare_and_fusion, bf16[16,3072,1]{1,0,2:T(8,128)(2,1)S(1)} %fusion.35), kind=kOutput, calls=%fused_computation.18 | convolution fusion | flops 339738624 | bytes 75620368 | tf_op jit(solution)/shard_map/bf,bfd->bd/dot_general | solution.py:99
  (92 shorter events, 22.5 us)
Async XLA Ops:
  7.2 37.3 %copy-start.14 = (u32[8]{0:T(128)S(1)}, u32[8]{0:T(128)}, u32[]{:S(2)}) copy-start(u32[8]{0:T(128)} %constant.75) | copy-start | bytes 100
  7.2 5.5 copy-start.7
  7.2 5.7 copy-start.11
  7.2 5.8 copy-start.9
  7.2 38.5 %copy-start.12 = (s32[16]{0:T(128)S(1)}, s32[16]{0:T(128)}, u32[]{:S(2)}) copy-start(s32[16]{0:T(128)} %param.29) | copy-start | bytes 196
  7.2 43.1 %copy-start.3 = (bf16[16,768]{1,0:T(8,128)(2,1)S(1)}, bf16[16,768]{1,0:T(8,128)(2,1)}, u32[]{:S(2)}) copy-start(bf16[16,768]{1,0:T(8,128)(2,1)} %param.21) | copy-start | bytes 73732
  7.2 43.5 %copy-start.4 = (s32[16,1024]{1,0:T(8,128)S(1)}, s32[16,1024]{1,0:T(8,128)}, u32[]{:S(2)}) copy-start(s32[16,1024]{1,0:T(8,128)} %param.27) | copy-start | bytes 196612
  7.2 44.1 %copy-start.6 = (f32[768]{0:T(1024)S(1)}, f32[768]{0:T(1024)}, u32[]{:S(2)}) copy-start(f32[768]{0:T(1024)} %param.30) | copy-start | bytes 9220
  7.2 44.1 %all-gather.12.cloned.1.call-start = ((), (), s32[]{:S(2)}) async-start(), calls=%async_computation.1 | async-start | bytes 1474560 | tf_op jit(solution)/shard_map/all_gather | solution.py:52
  8.0 45.3 %all-gather.14.cloned.1.call-start = ((), (), s32[]{:S(2)}) async-start(), calls=%async_computation.2 | async-start | bytes 1474560 | tf_op jit(solution)/shard_map/all_gather | solution.py:53
  8.7 50.6 %all-gather.10.cloned.1.call-start = ((), (), s32[]{:S(2)}) async-start(), calls=%async_computation | async-start | bytes 1474560 | tf_op jit(solution)/shard_map/all_gather | solution.py:51
  9.5 85.1 %all-gather.16.cloned.1.call-start = ((), (), s32[]{:S(2)}) async-start(), calls=%async_computation.3 | async-start | bytes 1474560 | tf_op jit(solution)/shard_map/all_gather | solution.py:54
  10.0 86.4 %all-gather.18.cloned.1.call-start = ((), (), s32[]{:S(2)}) async-start(), calls=%async_computation.4 | async-start | bytes 1474560 | tf_op jit(solution)/shard_map/all_gather | solution.py:55
  10.6 110.3 %all-gather.20.cloned.1.call-start = ((), (), s32[]{:S(2)}) async-start(), calls=%async_computation.5 | async-start | bytes 1474560 | tf_op jit(solution)/shard_map/all_gather | solution.py:56
  11.2 535.7 %all-gather.22.cloned.1.call-start = ((), (), s32[]{:S(2)}) async-start(), calls=%async_computation.6 | async-start | bytes 94371840 | tf_op jit(solution)/shard_map/all_gather | solution.py:58
  12.0 975.0 %all-gather.24.cloned.1.call-start = ((), (), s32[]{:S(2)}) async-start(), calls=%async_computation.7 | async-start | bytes 94371840 | tf_op jit(solution)/shard_map/all_gather | solution.py:59
  73.4 3.7 copy-start
  73.4 23.0 %copy-start.10 = (f32[768]{0:T(1024)S(1)}, f32[768]{0:T(1024)}, u32[]{:S(2)}) copy-start(f32[768]{0:T(1024)} %param.31) | copy-start | bytes 9220
  85.1 23.1 %copy-start.5 = (f32[16,1024]{1,0:T(8,128)S(1)}, f32[16,1024]{1,0:T(8,128)}, u32[]{:S(2)}) copy-start(f32[16,1024]{1,0:T(8,128)} %compare_select_fusion.2) | copy-start | bytes 196612
  108.2 14.6 %copy-start.8 = (f32[768]{0:T(1024)S(1)}, f32[768]{0:T(1024)}, u32[]{:S(2)}) copy-start(f32[768]{0:T(1024)} %param.32) | copy-start | bytes 9220
  122.8 0.9 copy-start.1
  1091.3 25.6 %copy-start.2 = (f32[16,768]{1,0:T(8,128)S(1)}, f32[16,768]{1,0:T(8,128)}, u32[]{:S(2)}) copy-start(f32[16,768]{1,0:T(8,128)} %copy-done.1) | copy-start | bytes 147460
  1091.3 25.6 %copy-start.13 = (f32[16]{0:T(128)S(1)}, f32[16]{0:T(128)}, u32[]{:S(2)}) copy-start(f32[16]{0:T(128)} %compare_select_fusion.4) | copy-start | bytes 196
Sparse Core Ops, SparseCore 0:
  9.6 17.5 all-gather.11
  28.7 14.5 all-gather.13
  44.9 14.4 all-gather.9
  60.7 14.4 all-gather.15
  76.6 14.4 all-gather.17
  92.5 14.4 all-gather.19
  108.6 438.3 all-gather.21
  548.5 438.4 all-gather.23
where the time goes:
time: 1130 us; the launch traced here: 1120 us
  waiting for transfers between devices  741 us (66%)
  local copies, waits for them, and re-layouts  238 us (21%)
  matrix products  93.9 us (8%)
  other arithmetic  20.8 us (2%)
  between operations  15.2 us (1%)
  blocking collectives  14.7 us (1%)
    all_gather x1, waiting for transfers between devices, decoder_block(): win_full = gather_ws(w_in, axis=2)  423 us
    all_gather x1, waiting for transfers between devices, decoder_block(): wout_full = gather_ws(w_out, axis=1)  309 us
    gather x4, local copies, waits for them, and re-layouts, decoder_block(): jnp.take(wout_full, expert_idx, axis=0)  104 us
    gather x4, local copies, waits for them, and re-layouts, decoder_block(): jnp.take(win_full, expert_idx, axis=0)  104 us
    dot_general x1, matrix products, decoder_block(): jnp.einsum('bd,bdf->bf', x_norm, jnp.take(win_full, expert_idx, axis=0),...  27.4 us
    dot_general x1, matrix products, decoder_block(): jnp.einsum('bf,bfd->bd', ffn_hidden, jnp.take(wout_full, expert_idx, axis...  25.6 us
  transfers between devices with their start and end apart: 8, of which 3 were waited for; matrix products, arithmetic and copies ran while one was open for 19% of the time, Pallas kernels for 0%

commit v1 on v0

v1 whole, which is shorter than its diff:
```python
import functools
import jax
import jax.numpy as jnp
from jax import lax
from jax.experimental import pallas as pl
from jax.experimental.pallas import tpu as pltpu
from jax.sharding import PartitionSpec as P

EPSILON = 1e-6
NEG_BIG = -1e30
F32 = jnp.float32
BF16 = jnp.bfloat16
MESH = pl.DeviceIdType.MESH
VMEM_SPEC = pl.BlockSpec(memory_space=pltpu.VMEM)
SMEM_SPEC = pl.BlockSpec(memory_space=pltpu.SMEM)
ANY_SPEC = pl.BlockSpec(memory_space=pl.ANY)
VMEM_MAX = 67_000_000
HEAD_PAD = 16


def rms_norm(hidden, scale):
    hid = hidden.astype(F32)
    inv = lax.rsqrt(jnp.mean(hid * hid, axis=-1, keepdims=True) + EPSILON)
    return (hid * inv * scale).astype(BF16)


def dot_nn(a, b):
    return lax.dot_general(a, b, (((1,), (0,)), ((), ())), preferred_element_type=F32)


def dot_nt(a, b):
    return lax.dot_general(a, b, (((1,), (1,)), ((), ())), preferred_element_type=F32)


def entry_barrier(me, n):
    sem = pltpu.get_barrier_semaphore()
    for k in range(1, n):
        pl.semaphore_signal(sem, inc=1, device_id={"ws": lax.rem(me + k, n)}, device_id_type=MESH)
    pl.semaphore_wait(sem, n - 1)


def start_exchange(me, n, src_of, dst, send_sem, recv_sem):
    copies = []
    for k in range(1, n):
        peer = lax.rem(me + k, n)
        copy = pltpu.make_async_remote_copy(
            src_ref=src_of(peer), dst_ref=dst, send_sem=send_sem.at[k - 1], recv_sem=recv_sem.at[k - 1],
            device_id={"ws": peer}, device_id_type=MESH)
        copy.start()
        copies.append(copy)
    return copies


def wait_all(copies):
    for copy in copies:
        copy.wait()


def my_columns(full, me, n, width):
    picked = full[:, 0:width]
    for j in range(1, n):
        picked = jnp.where(me == j, full[:, j * width:(j + 1) * width], picked)
    return picked


def qkv_kernel(n, h_ref, ln_ref, wq_ref, wk_ref, wv_ref, bias_ref, mask_ref,
               q_ref, k_ref, v_ref, hall_ref, brev_ref, lens_ref,
               hbuf, sendbuf, recvbuf, s1, r1, s2, r2):
    me = lax.axis_index("ws")
    rows, width = h_ref.shape
    cols = wq_ref.shape[0]
    entry_barrier(me, n)
    copies = start_exchange(me, n, lambda p: h_ref, hbuf.at[me], s1, r1)
    hbuf[me] = h_ref[...]
    lens_ref[...] = jnp.broadcast_to(jnp.sum(mask_ref[...], axis=1, keepdims=True), lens_ref.shape)
    length = bias_ref.shape[1]
    flip = (lax.broadcasted_iota(jnp.int32, (length, length), 0)
            + lax.broadcasted_iota(jnp.int32, (length, length), 1) == length - 1).astype(F32)
    brev_ref[...] = lax.dot_general(bias_ref[...], flip, (((1,), (0,)), ((), ())),
                                    precision=lax.Precision.HIGHEST, preferred_element_type=F32)
    wait_all(copies)
    hidden = hbuf[...].reshape(n * rows, width)
    hall_ref[...] = hidden
    x = rms_norm(hidden, ln_ref[...])
    for i, w in enumerate((wq_ref, wk_ref, wv_ref)):
        sendbuf[:, i] = dot_nt(x, w[...]).astype(BF16).reshape(n, rows, cols)
    copies = start_exchange(me, n, lambda p: sendbuf.at[p], recvbuf.at[me], s2, r2)
    recvbuf[me] = sendbuf[me]
    wait_all(copies)
    for i, o in enumerate((q_ref, k_ref, v_ref)):
        o[...] = jnp.concatenate([recvbuf[j, i] for j in range(n)], axis=1)


def block_rows(row, head_dim):
    width = row.shape[1]
    head = lax.broadcasted_iota(jnp.int32, (HEAD_PAD, width), 0)
    lane = lax.broadcasted_iota(jnp.int32, (HEAD_PAD, width), 1)
    return jnp.where(lane // head_dim == head, jnp.broadcast_to(row, (HEAD_PAD, width)), 0.0)


def softmax_rows(scores):
    top = jnp.max(scores, axis=-1, keepdims=True)
    e = jnp.exp(scores - top)
    return (e / jnp.sum(e, axis=-1, keepdims=True)).astype(BF16)


def self_kernel(heads, pos_ref, q_ref, k_ref, v_ref, brev_ref, sk_ref, sv_ref,
                ctx_ref, nk_ref, nv_ref,
                kbuf, vbuf, kt, vt, sbuf, pbuf, qf, cf, in_sem, out_sem):
    rows, width, length = kbuf.shape
    head_dim = width // heads

    def load(r, i):
        src, buf = ((sk_ref, kbuf), (sv_ref, vbuf))[i]
        return pltpu.make_async_copy(src.at[r], buf.at[r], in_sem.at[i, r])

    def save(r, i):
        buf, dst = ((kbuf, nk_ref), (vbuf, nv_ref))[i]
        return pltpu.make_async_copy(buf.at[r], dst.at[r], out_sem.at[i, r])

    for i in range(2):
        @pl.loop(0, rows)
        def _(r, i=i):
            load(r, i).start()

    pad = jnp.zeros((128 - rows, width), F32)
    kt[...] = jnp.transpose(jnp.concatenate([k_ref[...].astype(F32), pad], axis=0)).astype(BF16)
    vt[...] = jnp.transpose(jnp.concatenate([v_ref[...].astype(F32), pad], axis=0)).astype(BF16)
    qf[...] = q_ref[...].astype(F32)

    def insert(r, buf, cols):
        pos = pos_ref[0, r]
        tile = pos // 128
        at = pos - tile * 128
        row_i = lax.broadcasted_iota(jnp.int32, (128, 128), 0)
        lane_i = lax.broadcasted_iota(jnp.int32, (128, 128), 1)
        pick = jnp.where((row_i == r) & (lane_i == at), 1.0, 0.0).astype(BF16)
        new = dot_nn(cols[...], pick)
        view = buf.at[r, :, pl.ds(pl.multiple_of(tile * 128, 128), 128)]
        hit = lax.broadcasted_iota(jnp.int32, (width, 128), 1) == at
        view[...] = jnp.where(hit, new, view[...].astype(F32)).astype(BF16)

    @pl.loop(0, rows)
    def _(r):
        load(r, 0).wait()
        insert(r, kbuf, kt)
        q_blk = block_rows(qf[pl.ds(r, 1), :], head_dim).astype(BF16)
        sbuf[r] = dot_nn(q_blk, kbuf[r])
        save(r, 0).start()

    @pl.loop(0, rows)
    def _(r):
        pos = pos_ref[0, r]
        bias = pltpu.roll(brev_ref[...], lax.rem(pos + 1, length), 1)
        lane = lax.broadcasted_iota(jnp.int32, (HEAD_PAD, length), 1)
        pbuf[r] = softmax_rows(jnp.where(lane <= pos, sbuf[r] + bias, NEG_BIG))

    @pl.loop(0, rows)
    def _(r):
        load(r, 1).wait()
        insert(r, vbuf, vt)
        out = dot_nt(pbuf[r], vbuf[r])
        head = lax.broadcasted_iota(jnp.int32, (HEAD_PAD, width), 0)
        lane = lax.broadcasted_iota(jnp.int32, (HEAD_PAD, width), 1)
        cf[pl.ds(r, 1), :] = jnp.sum(jnp.where(lane // head_dim == head, out, 0.0), axis=0, keepdims=True)
        save(r, 1).start()

    ctx_ref[...] = cf[...].astype(BF16)
    for i in range(2):
        @pl.loop(0, rows)
        def _(r, i=i):
            save(r, i).wait()


def mid_kernel(n, ctx_ref, hall_ref, wo_ref, ln_ref, wq_ref,
               q_ref, h1_ref, cbuf, hpart, sendbuf, recvbuf, s1, r1, s2, r2, s3, r3):
    me = lax.axis_index("ws")
    rows, width = ctx_ref.shape
    cols = wo_ref.shape[0]
    entry_barrier(me, n)
    copies = start_exchange(me, n, lambda p: ctx_ref, cbuf.at[me], s1, r1)
    cbuf[me] = ctx_ref[...]
    mine = my_columns(hall_ref[...].astype(F32), me, n, cols)
    wait_all(copies)
    attn = dot_nt(cbuf[...].reshape(n * rows, width), wo_ref[...])
    hpart[me] = (mine + attn).astype(BF16)
    copies = start_exchange(me, n, lambda p: hpart.at[me], hpart.at[me], s2, r2)
    wait_all(copies)
    h1 = jnp.concatenate([hpart[j] for j in range(n)], axis=1)
    h1_ref[...] = h1
    x = rms_norm(h1, ln_ref[...])
    sendbuf[...] = dot_nt(x, wq_ref[...]).astype(BF16).reshape(n, rows, cols)
    copies = start_exchange(me, n, lambda p: sendbuf.at[p], recvbuf.at[me], s3, r3)
    recvbuf[me] = sendbuf[me]
    wait_all(copies)
    q_ref[...] = jnp.concatenate([recvbuf[j] for j in range(n)], axis=1)


def cross_kernel(heads, lens_ref, q_ref, mask_ref, ck_ref, cv_ref,
                 ctx_ref, kbuf, vbuf, sbuf, pbuf, qf, cf, in_sem):
    rows, width, length = kbuf.shape
    head_dim = width // heads
    tiles = length // 128

    def per_size(r, body):
        count = (lens_ref[r, 0] + 127) // 128
        for t in range(1, tiles + 1):
            @pl.when(count == t)
            def _(t=t):
                body(t * 128)

    def load(r, i, size):
        src, buf = ((ck_ref, kbuf), (cv_ref, vbuf))[i]
        return pltpu.make_async_copy(src.at[r, :, 0:size], buf.at[r, :, 0:size], in_sem.at[i, r])

    for i in range(2):
        @pl.loop(0, rows)
        def _(r, i=i):
            per_size(r, lambda size: load(r, i, size).start())

    qf[...] = q_ref[...].astype(F32)

    @pl.loop(0, rows)
    def _(r):
        q_blk = block_rows(qf[pl.ds(r, 1), :], head_dim).astype(BF16)

        def body(size):
            load(r, 0, size).wait()
            sbuf[r, :, 0:size] = dot_nn(q_blk, kbuf[r, :, 0:size])
        per_size(r, body)

    @pl.loop(0, rows)
    def _(r):
        keep = jnp.broadcast_to(mask_ref[pl.ds(r, 1), :], (HEAD_PAD, length)) == 1
        pbuf[r] = softmax_rows(jnp.where(keep, sbuf[r], NEG_BIG))

    @pl.loop(0, rows)
    def _(r):
        head = lax.broadcasted_iota(jnp.int32, (HEAD_PAD, width), 0)
        lane = lax.broadcasted_iota(jnp.int32, (HEAD_PAD, width), 1)

        def body(size):
            load(r, 1, size).wait()
            out = dot_nt(pbuf[r, :, 0:size], vbuf[r, :, 0:size])
            cf[pl.ds(r, 1), :] = jnp.sum(jnp.where(lane // head_dim == head, out, 0.0), axis=0, keepdims=True)
        per_size(r, body)

    ctx_ref[...] = cf[...].astype(BF16)


def ffn_kernel(n, ctx_ref, h1_ref, wo_ref, ln_ref, wr_ref, idx_ref, win_ref, wout_ref,
               out_ref, cbuf, hpart, rbuf, ibuf, xbuf, mbuf, wi, wo, acc, part, own, ybuf,
               s1, r1, s2, r2, s3, r3, s4, r4, s5, r5, wi_sem, wo_sem):
    me = lax.axis_index("ws")
    rows, width = ctx_ref.shape
    cols = wo_ref.shape[0]
    experts = win_ref.shape[0]
    total = n * rows
    capacity = (2 * total + experts - 1) // experts

    def load(e, i):
        src, buf, sem = ((win_ref, wi, wi_sem), (wout_ref, wo, wo_sem))[i]
        return pltpu.make_async_copy(src.at[e], buf.at[e], sem.at[e])

    @pl.loop(0, experts)
    def _(e):
        load(e, 0).start()
        load(e, 1).start()

    entry_barrier(me, n)
    first = (start_exchange(me, n, lambda p: ctx_ref, cbuf.at[me], s1, r1)
             + start_exchange(me, n, lambda p: idx_ref, ibuf.at[me], s2, r2)
             + start_exchange(me, n, lambda p: wr_ref, rbuf.at[me], s3, r3))
    cbuf[me] = ctx_ref[...]
    ibuf[me] = idx_ref[...]
    rbuf[me] = wr_ref[...]
    mine = my_columns(h1_ref[...].astype(F32), me, n, cols)
    wait_all(first)
    attn = dot_nt(cbuf[...].reshape(total, width), wo_ref[...])
    hpart[me] = (mine + attn).astype(BF16)
    copies = start_exchange(me, n, lambda p: hpart.at[me], hpart.at[me], s4, r4)

    idx_row = jnp.concatenate([ibuf[j] for j in range(n)], axis=1)
    grid_i = lax.broadcasted_iota(jnp.int32, (total, total), 0)
    grid_j = lax.broadcasted_iota(jnp.int32, (total, total), 1)
    row_b = jnp.broadcast_to(idx_row, (total, total))
    idx_col = jnp.sum(jnp.where(grid_i == grid_j, row_b, 0), axis=1, keepdims=True)
    earlier = (row_b == idx_col) & (grid_j < grid_i)
    slot = jnp.sum(earlier.astype(jnp.int32), axis=1, keepdims=True)
    target = jnp.where(slot < capacity, idx_col, -1)
    mbuf[...] = jnp.broadcast_to(target, mbuf.shape)

    wait_all(copies)
    h2 = jnp.concatenate([hpart[j] for j in range(n)], axis=1)
    x = rms_norm(h2, ln_ref[...])
    xbuf[...] = x
    own[...] = h2.reshape(n, rows, width)
    acc[...] = jnp.zeros_like(acc)

    @pl.loop(0, experts)
    def _(e):
        load(e, 0).wait()
        u = jnp.maximum(dot_nn(xbuf[...], wi[e]), 0.0)
        hit = jnp.broadcast_to(mbuf[:, 0:1], u.shape) == e
        u = jnp.where(hit, u, 0.0).astype(BF16)
        load(e, 1).wait()
        acc[...] += dot_nn(u, wo[e])

    part[...] = acc[...].reshape(n, rows, width)
    copies = start_exchange(me, n, lambda p: part.at[p], ybuf.at[me], s5, r5)
    ybuf[me] = part[me]

    my_rows = pl.ds(pl.multiple_of(me * rows, rows), rows)
    router = jnp.concatenate([rbuf[j] for j in range(n)], axis=0)
    logits = lax.dot_general(xbuf[my_rows, :].astype(F32), router, (((1,), (1,)), ((), ())),
                             precision=lax.Precision.HIGHEST, preferred_element_type=F32)
    probs = jnp.exp(logits - jnp.max(logits, axis=-1, keepdims=True))
    probs = probs / jnp.sum(probs, axis=-1, keepdims=True)
    chosen = lax.broadcasted_iota(jnp.int32, (rows, experts), 1) == mbuf[my_rows, :][:, 0:experts]
    gate = jnp.sum(jnp.where(chosen, probs, 0.0), axis=-1, keepdims=True)
    wait_all(copies)
    y = ybuf[0]
    for j in range(1, n):
        y = y + ybuf[j]
    out_ref[...] = (own[me].astype(F32) + y.astype(BF16).astype(F32) * gate).astype(BF16)


def call(body, out_shape, in_specs, out_specs, scratch, collective=None, flops=1_000_000, moved=1_000_000, vmem=VMEM_MAX):
    params = dict(vmem_limit_bytes=vmem)
    if collective is not None:
        params.update(collective_id=collective, has_side_effects=True)
    return pl.pallas_call(
        body, out_shape=out_shape, in_specs=in_specs, out_specs=out_specs, scratch_shapes=scratch,
        compiler_params=pltpu.CompilerParams(**params),
        cost_estimate=pl.CostEstimate(flops=flops, bytes_accessed=moved, transcendentals=0))


def solution(mesh):
    n = mesh.shape['ws']
    row_axes = ('dp', 'ws')
    row_vec = P(row_axes)
    row_mat = P(row_axes, None)
    cache_spec = P(row_axes, None, None, None)
    col_split = P(None, 'ws')
    in_specs = (row_mat, cache_spec, cache_spec, cache_spec, cache_spec, row_vec, row_mat, P(None, None), row_vec,
                P(None), P(None), P(None), col_split, col_split, col_split, col_split, col_split, col_split,
                col_split, P(None, None, 'ws'), P(None, 'ws', None))
    out_specs = (row_mat, cache_spec, cache_spec)
    dma = pltpu.SemaphoreType.DMA

    def decoder_block(hidden, self_k, self_v, cross_k, cross_v, positions, enc_mask, rel_bias, expert_idx,
                      ln_self, ln_cross, ln_ffn, wq_self, wk_self, wv_self, wo_self, wq_cross, wo_cross,
                      w_router, w_in, w_out):
        rows, width = hidden.shape
        heads, length = rel_bias.shape
        head_dim = width // heads
        source = enc_mask.shape[1]
        cols = wq_self.shape[1]
        experts, _, units = w_in.shape
        total = n * rows
        sds = jax.ShapeDtypeStruct

        def flat(cache):
            return jnp.swapaxes(cache, 2, 3).reshape(rows, width, cache.shape[2])

        bias16 = jnp.pad(rel_bias, ((0, HEAD_PAD - heads), (0, 0)))
        sems = [dma((n - 1,))]
        q, k, v, hall, brev, lens = call(
            functools.partial(qkv_kernel, n),
            [sds((rows, width), BF16)] * 3 + [sds((total, width), BF16), sds((HEAD_PAD, length), F32), sds((rows, 128), jnp.int32)],
            [VMEM_SPEC] * 7, [VMEM_SPEC] * 6,
            [pltpu.VMEM((n, rows, width), BF16), pltpu.VMEM((n, 3, rows, cols), BF16), pltpu.VMEM((n, 3, rows, cols), BF16)] + sems * 4,
            collective=0, vmem=16_000_000,
        )(hidden, ln_self[None, :], wq_self.T, wk_self.T, wv_self.T, bias16, enc_mask)

        ctx, new_k, new_v = call(
            functools.partial(self_kernel, heads),
            [sds((rows, width), BF16)] + [sds((rows, width, length), BF16)] * 2,
            [SMEM_SPEC] + [VMEM_SPEC] * 4 + [ANY_SPEC] * 2, [VMEM_SPEC] + [ANY_SPEC] * 2,
            [pltpu.VMEM((rows, width, length), BF16)] * 2 + [pltpu.VMEM((width, 128), BF16)] * 2
            + [pltpu.VMEM((rows, HEAD_PAD, length), F32), pltpu.VMEM((rows, HEAD_PAD, length), BF16),
               pltpu.VMEM((rows, width), F32), pltpu.VMEM((rows, width), F32), dma((2, rows)), dma((2, rows))],
        )(positions[None, :], q, k, v, brev, flat(self_k), flat(self_v))

        qc, h1 = call(
            functools.partial(mid_kernel, n),
            [sds((rows, width), BF16), sds((total, width), BF16)],
            [VMEM_SPEC] * 5, [VMEM_SPEC] * 2,
            [pltpu.VMEM((n, rows, width), BF16), pltpu.VMEM((n, total, cols), BF16),
             pltpu.VMEM((n, rows, cols), BF16), pltpu.VMEM((n, rows, cols), BF16)] + sems * 6,
            collective=1, vmem=16_000_000,
        )(ctx, hall, wo_self.T, ln_cross[None, :], wq_cross.T)

        ctx2 = call(
            functools.partial(cross_kernel, heads),
            sds((rows, width), BF16),
            [SMEM_SPEC] + [VMEM_SPEC] * 2 + [ANY_SPEC] * 2, VMEM_SPEC,
            [pltpu.VMEM((rows, width, source), BF16)] * 2
            + [pltpu.VMEM((rows, HEAD_PAD, source), F32), pltpu.VMEM((rows, HEAD_PAD, source), BF16),
               pltpu.VMEM((rows, width), F32), pltpu.VMEM((rows, width), F32), dma((2, rows))],
        )(lens, qc, enc_mask, flat(cross_k), flat(cross_v))

        out = call(
            functools.partial(ffn_kernel, n),
            sds((rows, width), BF16),
            [VMEM_SPEC] * 6 + [ANY_SPEC] * 2, VMEM_SPEC,
            [pltpu.VMEM((n, rows, width), BF16), pltpu.VMEM((n, total, cols), BF16),
             pltpu.VMEM((n, experts // n, width), F32), pltpu.VMEM((n, 1, rows), jnp.int32),
             pltpu.VMEM((total, width), BF16), pltpu.VMEM((total, 128), jnp.int32),
             pltpu.VMEM((experts, width, units), BF16), pltpu.VMEM((experts, units, width), BF16),
             pltpu.VMEM((total, width), F32), pltpu.VMEM((n, rows, width), F32), pltpu.VMEM((n, rows, width), BF16),
             pltpu.VMEM((n, rows, width), F32)]
            + sems * 10 + [dma((experts,)), dma((experts,))],
            collective=2,
        )(ctx2, h1, wo_cross.T, ln_ffn[None, :], w_router.T, expert_idx[None, :], w_in, w_out)

        def unflat(cache):
            return jnp.swapaxes(cache.reshape(rows, heads, head_dim, length), 2, 3)

        return out, unflat(new_k), unflat(new_v)

    return jax.shard_map(decoder_block, mesh=mesh, in_specs=in_specs, out_specs=out_specs, check_vma=False)
```

time: 1130 us -> 105 us (0.09)
  waiting for transfers between devices: 741 us -> 0 us
  local copies, waits for them, and re-layouts: 238 us -> 16.3 us
  matrix products: 93.9 us -> 0 us
  Pallas kernels: 0 us -> 86.6 us
  other arithmetic: 20.8 us -> 0 us
  blocking collectives: 14.7 us -> 0 us
  between operations: 15.2 us -> 0.74 us
    all_gather x8 -> x0, waiting for transfers between devices: 736 us -> none  [the longest x1 423 us: decoder_block(): win_full = gather_ws(w_in, axis=2)]
    gather x9 -> x0, local copies, waits for them, and re-layouts: 229 us -> none  [the longest x4 104 us: decoder_block(): jnp.take(wout_full, expert_idx, axis=0)]
    dot_general x13 -> x0, matrix products: 93.9 us -> none  [the longest x1 27.4 us: decoder_block(): jnp.einsum('bd,bdf->bf', x_norm, jnp.take(win_full, expert_idx, axis=0),...]
    pallas_call x0 -> x5, Pallas kernels: none -> 86.6 us  [the longest x1 25.9 us: decoder_block(): call(functools.partial(ffn_kernel, n), sds((rows, width), BF16), [VMEM_SP...]
    select_n x5 -> x0, other arithmetic: 13.5 us -> none  [the longest x1 12.2 us: decoder_block(): new_self_v = jnp.where(write_mask, v_new[:, :, None, :], self_v)]
  transfers between devices with their start and end apart: 8 -> 0, of which waited for: 3 -> 0; matrix products, arithmetic and copies ran while one was open for 19% -> 0% of each run, Pallas kernels for 0% -> 0%
where the time goes in v1:
time: 105 us; the launch traced here: 104 us
  Pallas kernels  86.6 us (82%)
  local copies, waits for them, and re-layouts  16.3 us (16%)
    pallas_call x1, Pallas kernels, decoder_block(): call(functools.partial(ffn_kernel, n), sds((rows, width), BF16), [VMEM_SP...  25.9 us
    pallas_call x1, Pallas kernels, decoder_block(): call(functools.partial(self_kernel, heads), [sds((rows, width), BF16)] +...  23.9 us
    pallas_call x1, Pallas kernels, decoder_block(): call(functools.partial(cross_kernel, heads), sds((rows, width), BF16), [S...  16.5 us
    unnamed x39, local copies, waits for them, and re-layouts  14.2 us
    pallas_call x1, Pallas kernels, decoder_block(): call(functools.partial(mid_kernel, n), [sds((rows, width), BF16), sds((to...  10.6 us
    pallas_call x1, Pallas kernels, decoder_block(): call(functools.partial(qkv_kernel, n), [sds((rows, width), BF16)] * 3 + [...  9.65 us

profile of v1, /device:TPU:0, one launch (start us, length us, event | category | flops | bytes accessed | tf_op | source)
XLA Modules:
  0.0 103.5 jit_solution(2502747388228573503)
XLA Ops:
  0.6 0.7 broadcast_in_dim.15.ln_ref
  1.3 0.7 pad.4.bias_ref
  2.1 1.0 copy-done
  3.0 1.0 copy-done.1
  4.0 1.0 copy-done.2
  5.0 0.8 copy-done.5
  5.8 0.7 copy-done.11
  6.5 9.6 %shard_map.220 = (bf16[16,768]{1,0:T(8,128)(2,1)S(1)}, bf16[16,768]{1,0:T(8,128)(2,1)S(1)}, bf16[16,768]{1,0:T(8,128)(2,1)S(1)}, bf16[64,768]{1,0:T(8,128)(2,1)S...) custom-call(bf16[16,768]{1,0:T(8,128)(2,1)S(1)} %copy-done.11, f32[1,768]{1,0:T(1,128)S(1)} %broadcast_in_dim.15.ln_ref, ...), custom_call_target="tpu_custom_call" | custom-call | flops 1000000 | bytes 1000000 | tf_op jit(solution)/shard_map/pallas_call | solution.py:368
  16.2 0.6 copy-done.6
  16.8 0.6 copy-done.12
  17.4 0.6 copy-done.13
  18.1 0.6 copy-done.14
  18.6 0.6 copy-done.15
  19.8 23.9 %shard_map.221 = (bf16[16,768]{1,0:T(8,128)(2,1)}, bf16[16,768,384]{2,1,0:T(8,128)(2,1)}, bf16[16,768,384]{2,1,0:T(8,128)(2,1)}) custom-call(s32[1,16]{1,0:T(1,128)} %bitcast.38, bf16[16,768]{1,0:T(8,128)(2,1)} %copy-done.12, bf16[16,768]{1,0:T(8,128)(2,1)} %copy-done.13, bf16[16,768]{1,0:T(8,128)(2,1)} %copy-done.14, f32[16,384]{1,0:T(8,128)} %copy-done.15, ...), custom_call_target="tpu_custom_call" | custom-call | flops 1000000 | bytes 1000000 | tf_op jit(solution)/shard_map/pallas_call | solution.py:376
  43.8 1.0 copy-done.3
  44.8 1.0 copy-done.4
  45.7 0.9 copy-done.7
  46.6 0.7 copy-done.10
  47.4 10.6 %shard_map.222 = (bf16[16,768]{1,0:T(8,128)(2,1)S(1)}, bf16[64,768]{1,0:T(8,128)(2,1)S(1)}) custom-call(bf16[16,768]{1,0:T(8,128)(2,1)S(1)} %copy-done.10, bf16[64,768]{1,0:T(8,128)(2,1)S(1)} %copy-done.7, bf16[192,768]{1,0:T(8,128)(2,1)S(1)} %bitcast.30, f32[1,768]{1,0:T(1,128)S(1)} %broadcast_in_dim.17.ln_ref, bf16[192,768]{1,0:T(8,128)(2,1)S(1)} %bitcast.31), custom_call_target="tpu_custom_call" | custom-call | flops 1000000 | bytes 1000000 | tf_op jit(solution)/shard_map/pallas_call | solution.py:385
  58.0 0.6 copy-done.8
  58.6 0.6 copy-done.9
  59.2 16.5 %shard_map.223.ctx_ref = bf16[16,768]{1,0:T(8,128)(2,1)} custom-call(s32[16,128]{1,0:T(8,128)} %copy-done.16, bf16[16,768]{1,0:T(8,128)(2,1)} %copy-done.9, s32[16,1024]{1,0:T(8,128)} %mask_ref.3, bf16[16,768,1024]{2,1,0:T(8,128)(2,1)} %bitcast.32, bf16[16,768,1024]{2,1,0:T(8,128)(2,1)} %bitcast.33), custom_call_target="tpu_custom_call" | custom-call | flops 1000000 | bytes 1000000 | tf_op jit(solution)/shard_map/pallas_call | solution.py:394
  76.3 25.9 %shard_map.224 = bf16[16,768]{1,0:T(8,128)(2,1)} custom-call(bf16[16,768]{1,0:T(8,128)(2,1)} %shard_map.223.ctx_ref, bf16[64,768]{1,0:T(8,128)(2,1)} %copy-done.8, bf16[192,768]{1,0:T(8,128)(2,1)} %bitcast.36, f32[1,768]{1,0:T(1,128)} %broadcast_in_dim.18.ln_ref, f32[4,768]{1,0:T(4,128)} %bitcast.37, s32[1,16]{1,0:T(1,128)} %bitcast.39, ...), custom_call_target="tpu_custom_call" | custom-call | flops 1000000 | bytes 1000000 | tf_op jit(solution)/shard_map/pallas_call | solution.py:403
  102.2 1.3 %copy.25 = bf16[16,768]{1,0:T(8,128)(2,1)} copy(bf16[16,768]{1,0:T(8,128)(2,1)} %shard_map.224) | data formatting | bytes 49152
  (24 shorter events, 1.2 us)
Async XLA Ops:
  0.6 43.1 %copy-start.17 = (f32[768]{0:T(1024)S(1)}, f32[768]{0:T(1024)}, u32[]{:S(2)}) copy-start(f32[768]{0:T(1024)} %param.31) | copy-start | bytes 9220
  2.1 1.0 copy-start
  3.0 1.0 copy-start.1
  4.0 1.0 copy-start.2
  5.0 0.8 copy-start.5
  5.8 0.7 copy-start.11
  16.2 0.6 copy-start.6
  16.8 0.6 copy-start.12
  17.4 0.6 copy-start.13
  18.0 0.6 copy-start.14
  18.6 0.6 copy-start.15
  19.2 0.6 copy-start.16
  43.8 1.0 copy-start.3
  44.8 1.0 copy-start.4
  45.7 0.9 copy-start.7
  46.6 0.7 copy-start.10
  58.0 0.6 copy-start.8
  58.6 0.6 copy-start.9
  59.2 16.5 %copy-start.18 = (f32[768]{0:T(1024)S(1)}, f32[768]{0:T(1024)}, u32[]{:S(2)}) copy-start(f32[768]{0:T(1024)} %param.32) | copy-start | bytes 9220

commit v2 on v1

v2 whole, which is shorter than its diff:
```python
import functools
import jax
import jax.numpy as jnp
from jax import lax
from jax.experimental import pallas as pl
from jax.experimental.pallas import tpu as pltpu
from jax.sharding import PartitionSpec as P

EPSILON = 1e-6
NEG_BIG = -1e30
F32 = jnp.float32
BF16 = jnp.bfloat16
MESH = pl.DeviceIdType.MESH
VMEM_SPEC = pl.BlockSpec(memory_space=pltpu.VMEM)
SMEM_SPEC = pl.BlockSpec(memory_space=pltpu.SMEM)
HBM_SPEC = pl.BlockSpec(memory_space=pltpu.HBM)
VMEM_MAX = 67_000_000
HEAD_PAD = 16


def rms_norm(hidden, scale):
    hid = hidden.astype(F32)
    inv = lax.rsqrt(jnp.mean(hid * hid, axis=-1, keepdims=True) + EPSILON)
    return (hid * inv * scale).astype(BF16)


def dot_nn(a, b):
    return lax.dot_general(a, b, (((1,), (0,)), ((), ())), preferred_element_type=F32)


def dot_nt(a, b):
    return lax.dot_general(a, b, (((1,), (1,)), ((), ())), preferred_element_type=F32)


def entry_barrier(me, n):
    sem = pltpu.get_barrier_semaphore()
    for k in range(1, n):
        pl.semaphore_signal(sem, inc=1, device_id={"ws": lax.rem(me + k, n)}, device_id_type=MESH)
    pl.semaphore_wait(sem, n - 1)


def start_exchange(me, n, src_of, dst, send_sem, recv_sem):
    copies = []
    for k in range(1, n):
        peer = lax.rem(me + k, n)
        copy = pltpu.make_async_remote_copy(
            src_ref=src_of(peer), dst_ref=dst, send_sem=send_sem.at[k - 1], recv_sem=recv_sem.at[k - 1],
            device_id={"ws": peer}, device_id_type=MESH)
        copy.start()
        copies.append(copy)
    return copies


def wait_all(copies):
    for copy in copies:
        copy.wait()


def my_columns(full, me, n, width):
    picked = full[:, 0:width]
    for j in range(1, n):
        picked = jnp.where(me == j, full[:, j * width:(j + 1) * width], picked)
    return picked


def fetch(pairs, sem):
    copies = [pltpu.make_async_copy(src, dst, sem.at[i]) for i, (src, dst) in enumerate(pairs)]
    for copy in copies:
        copy.start()
    return copies


def qkv_kernel(n, h_hbm, ln_hbm, wq_hbm, wk_hbm, wv_hbm, bias_hbm, mask_hbm,
               q_ref, k_ref, v_ref, hall_ref, brev_ref, lens_ref,
               h_ref, ln_ref, w_ref, bias_ref, mask_ref, hbuf, sendbuf, recvbuf, s1, r1, s2, r2, in_sem):
    me = lax.axis_index("ws")
    rows, width = h_ref.shape
    cols = w_ref.shape[1]
    loads = fetch([(h_hbm, h_ref), (ln_hbm, ln_ref), (bias_hbm, bias_ref), (mask_hbm, mask_ref)]
                  + [(w, w_ref.at[i]) for i, w in enumerate((wq_hbm, wk_hbm, wv_hbm))], in_sem)
    entry_barrier(me, n)
    loads[0].wait()
    copies = start_exchange(me, n, lambda p: h_ref, hbuf.at[me], s1, r1)
    hbuf[me] = h_ref[...]
    for load in loads[1:]:
        load.wait()
    lens_ref[...] = jnp.broadcast_to(jnp.sum(mask_ref[...], axis=1, keepdims=True), lens_ref.shape)
    heads, length = bias_ref.shape
    flip = (lax.broadcasted_iota(jnp.int32, (length, length), 0)
            + lax.broadcasted_iota(jnp.int32, (length, length), 1) == length - 1).astype(F32)
    brev_ref[...] = jnp.zeros_like(brev_ref)
    brev_ref[0:heads, :] = lax.dot_general(bias_ref[...], flip, (((1,), (0,)), ((), ())),
                                           precision=lax.Precision.HIGHEST, preferred_element_type=F32)
    wait_all(copies)
    hidden = hbuf[...].reshape(n * rows, width)
    hall_ref[...] = hidden
    x = rms_norm(hidden, ln_ref[...].reshape(1, width))
    for i in range(3):
        sendbuf[:, i] = dot_nt(x, w_ref[i]).astype(BF16).reshape(n, rows, cols)
    copies = start_exchange(me, n, lambda p: sendbuf.at[p], recvbuf.at[me], s2, r2)
    recvbuf[me] = sendbuf[me]
    wait_all(copies)
    for i, o in enumerate((q_ref, k_ref, v_ref)):
        o[...] = jnp.concatenate([recvbuf[j, i] for j in range(n)], axis=1)


def head_mask(shape, head_dim):
    head = lax.broadcasted_iota(jnp.int32, shape, 0)
    return lax.broadcasted_iota(jnp.int32, shape, 1) // head_dim == head


def spread_heads(q_ref, qblk, head_dim):
    rows, width = q_ref.shape
    q = q_ref[...].astype(F32)
    keep = head_mask((HEAD_PAD, width), head_dim)
    for r in range(rows):
        qblk[r] = jnp.where(keep, jnp.broadcast_to(q[r:r + 1], (HEAD_PAD, width)), 0.0).astype(BF16)


def softmax_rows(scores):
    top = jnp.max(scores, axis=-1, keepdims=True)
    e = jnp.exp(scores - top)
    return (e / jnp.sum(e, axis=-1, keepdims=True)).astype(BF16).astype(F32)


def weighted_values(prob, value, heads, head_dim, length):
    parts = []
    for h in range(heads):
        total = None
        for t in range(length // 128):
            lanes = slice(t * 128, (t + 1) * 128)
            term = value[h * head_dim:(h + 1) * head_dim, lanes].astype(F32) * prob[h:h + 1, lanes]
            total = term if total is None else total + term
        parts.append(total)
    return jnp.sum(jnp.transpose(jnp.concatenate(parts, axis=0)), axis=0, keepdims=True)


def self_kernel(heads, pos_hbm, q_ref, k_ref, v_ref, brev_ref, sk_ref, sv_ref,
                ctx_ref, nk_ref, nv_ref,
                kbuf, vbuf, kt, vt, s0, s1, p0, p1, qblk, cf, in_sem, out_sem, pos_ref, pos_sem):
    rows, width, length = kbuf.shape
    head_dim = width // heads
    scalars = pltpu.make_async_copy(pos_hbm, pos_ref, pos_sem)
    scalars.start()

    def load(r, i):
        src, buf = ((sk_ref, kbuf), (sv_ref, vbuf))[i]
        return pltpu.make_async_copy(src.at[r], buf.at[r], in_sem.at[i, r])

    def save(r, i):
        buf, dst = ((kbuf, nk_ref), (vbuf, nv_ref))[i]
        return pltpu.make_async_copy(buf.at[r], dst.at[r], out_sem.at[i, r])

    for r in range(rows):
        load(r, 0).start()
        load(r, 1).start()

    pad = jnp.zeros((128 - rows, width), F32)
    kt[...] = jnp.transpose(jnp.concatenate([k_ref[...].astype(F32), pad], axis=0))
    vt[...] = jnp.transpose(jnp.concatenate([v_ref[...].astype(F32), pad], axis=0))
    spread_heads(q_ref, qblk, head_dim)
    sbufs, pbufs = (s0, s1), (p0, p1)
    scalars.wait()

    def insert(r, buf, cols):
        pos = pos_ref[r]
        tile = pos // 128
        at = pos - tile * 128
        new = jnp.broadcast_to(cols[:, r:r + 1], (width, 128))
        view = buf.at[r, :, pl.ds(pl.multiple_of(tile * 128, 128), 128)]
        hit = lax.broadcasted_iota(jnp.int32, (width, 128), 1) == at
        view[...] = jnp.where(hit, new, view[...].astype(F32)).astype(BF16)

    def softmax(r):
        pos = pos_ref[r]
        bias = pltpu.roll(brev_ref[...], lax.rem(pos + 1, length), 1)
        lane = lax.broadcasted_iota(jnp.int32, (HEAD_PAD, length), 1)
        pbufs[r % 2][...] = softmax_rows(jnp.where(lane <= pos, sbufs[r % 2][...] + bias, NEG_BIG))

    for step in range(rows + 3):
        r = step
        if r < rows:
            load(r, 0).wait()
            load(r, 1).wait()
        if step >= 3:
            done = step - 3
            cf[done:done + 1, :] = weighted_values(pbufs[done % 2], vbuf.at[done], heads, head_dim, length)
        if 2 <= step < rows + 2:
            softmax(step - 2)
        if 1 <= step < rows + 1:
            sbufs[(step - 1) % 2][...] = dot_nn(qblk[step - 1], kbuf[step - 1])
        if r < rows:
            insert(r, kbuf, kt)
            insert(r, vbuf, vt)
        if 1 <= step < rows + 1:
            save(step - 1, 0).start()
            save(step - 1, 1).start()

    ctx_ref[...] = cf[...].astype(BF16)
    for r in range(rows):
        save(r, 0).wait()
        save(r, 1).wait()


def mid_kernel(n, ctx_ref, hall_ref, wo_hbm, ln_hbm, wq_hbm,
               q_ref, h1_ref, wo_ref, ln_ref, wq_ref, in_sem, cbuf, hpart, sendbuf, recvbuf, s1, r1, s2, r2, s3, r3):
    me = lax.axis_index("ws")
    rows, width = ctx_ref.shape
    cols = wo_ref.shape[0]
    loads = fetch([(wo_hbm, wo_ref), (ln_hbm, ln_ref), (wq_hbm, wq_ref)], in_sem)
    entry_barrier(me, n)
    copies = start_exchange(me, n, lambda p: ctx_ref, cbuf.at[me], s1, r1)
    cbuf[me] = ctx_ref[...]
    mine = my_columns(hall_ref[...].astype(F32), me, n, cols)
    wait_all(loads)
    wait_all(copies)
    attn = dot_nt(cbuf[...].reshape(n * rows, width), wo_ref[...])
    hpart[me] = (mine + attn).astype(BF16)
    copies = start_exchange(me, n, lambda p: hpart.at[me], hpart.at[me], s2, r2)
    wait_all(copies)
    h1 = jnp.concatenate([hpart[j] for j in range(n)], axis=1)
    h1_ref[...] = h1
    x = rms_norm(h1, ln_ref[...].reshape(1, width))
    sendbuf[...] = dot_nt(x, wq_ref[...]).astype(BF16).reshape(n, rows, cols)
    copies = start_exchange(me, n, lambda p: sendbuf.at[p], recvbuf.at[me], s3, r3)
    recvbuf[me] = sendbuf[me]
    wait_all(copies)
    q_ref[...] = jnp.concatenate([recvbuf[j] for j in range(n)], axis=1)


def cross_kernel(heads, lens_ref, q_ref, mask_ref, ck_ref, cv_ref,
                 ctx_ref, kbuf, vbuf, s0, s1, p0, p1, qblk, cf, in_sem):
    rows, width, length = kbuf.shape
    head_dim = width // heads
    tiles = length // 128

    def tile_count(r):
        return (lens_ref[r, 0] + 127) // 128

    def per_size(r, body):
        count = tile_count(r)
        for t in range(1, tiles + 1):
            @pl.when(count == t)
            def _(t=t):
                body(t * 128)

    def load(r, i, size):
        src, buf = ((ck_ref, kbuf), (cv_ref, vbuf))[i]
        return pltpu.make_async_copy(src.at[r, :, 0:size], buf.at[r, :, 0:size], in_sem.at[i, r])

    @pl.loop(0, rows)
    def _(r):
        per_size(r, lambda size: load(r, 0, size).start())
        per_size(r, lambda size: load(r, 1, size).start())

    spread_heads(q_ref, qblk, head_dim)

    @pl.loop(0, rows)
    def _(r):
        @pl.loop(tile_count(r), tiles)
        def _(t):
            vbuf[r, :, pl.ds(pl.multiple_of(t * 128, 128), 128)] = jnp.zeros((width, 128), BF16)

    sbufs, pbufs = (s0, s1), (p0, p1)

    for step in range(rows + 2):
        if step < rows:
            per_size(step, lambda size: load(step, 0, size).wait())
        if step >= 2:
            per_size(step - 2, lambda size: load(step - 2, 1, size).wait())
            done = step - 2
            cf[done:done + 1, :] = weighted_values(pbufs[done % 2], vbuf.at[done], heads, head_dim, length)
        if 1 <= step < rows + 1:
            r = step - 1
            keep = jnp.broadcast_to(mask_ref[r:r + 1, :], (HEAD_PAD, length)) == 1
            pbufs[r % 2][...] = softmax_rows(jnp.where(keep, sbufs[r % 2][...], NEG_BIG))
        if step < rows:
            sbufs[step % 2][...] = dot_nn(qblk[step], kbuf[step])

    ctx_ref[...] = cf[...].astype(BF16)


def ffn_kernel(n, ctx_ref, h1_ref, wo_hbm, ln_hbm, wr_hbm, idx_hbm, win_ref, wout_ref,
               out_ref, cbuf, hpart, rbuf, ibuf, xbuf, mbuf, wi, wo, u0, u1, part, own, ybuf,
               s1, r1, s2, r2, s3, r3, s4, r4, s5, r5, wi_sem, wo_sem,
               wo_ref, ln_ref, wr_ref, idx_ref, in_sem):
    me = lax.axis_index("ws")
    rows, width = ctx_ref.shape
    cols = wo_ref.shape[0]
    experts = win_ref.shape[0]
    total = n * rows
    capacity = (2 * total + experts - 1) // experts

    def load(e, i):
        src, buf, sem = ((win_ref, wi, wi_sem), (wout_ref, wo, wo_sem))[i]
        return pltpu.make_async_copy(src.at[e], buf.at[e], sem.at[e])

    loads = fetch([(idx_hbm, idx_ref), (wr_hbm, wr_ref), (wo_hbm, wo_ref), (ln_hbm, ln_ref)], in_sem)

    @pl.loop(0, experts)
    def _(e):
        load(e, 0).start()
        load(e, 1).start()

    entry_barrier(me, n)
    wait_all(loads)
    first = (start_exchange(me, n, lambda p: ctx_ref, cbuf.at[me], s1, r1)
             + start_exchange(me, n, lambda p: idx_ref, ibuf.at[me], s2, r2)
             + start_exchange(me, n, lambda p: wr_ref, rbuf.at[me], s3, r3))
    cbuf[me] = ctx_ref[...]
    ibuf[me] = idx_ref[...]
    rbuf[me] = wr_ref[...]
    mine = my_columns(h1_ref[...].astype(F32), me, n, cols)
    wait_all(first)
    attn = dot_nt(cbuf[...].reshape(total, width), wo_ref[...])
    hpart[me] = (mine + attn).astype(BF16)
    copies = start_exchange(me, n, lambda p: hpart.at[me], hpart.at[me], s4, r4)

    idx_row = jnp.concatenate([ibuf[j] for j in range(n)], axis=1)
    grid_i = lax.broadcasted_iota(jnp.int32, (total, total), 0)
    grid_j = lax.broadcasted_iota(jnp.int32, (total, total), 1)
    row_b = jnp.broadcast_to(idx_row, (total, total))
    idx_col = jnp.sum(jnp.where(grid_i == grid_j, row_b, 0), axis=1, keepdims=True)
    earlier = (row_b == idx_col) & (grid_j < grid_i)
    slot = jnp.sum(earlier.astype(jnp.int32), axis=1, keepdims=True)
    target = jnp.where(slot < capacity, idx_col, -1)
    mbuf[...] = jnp.broadcast_to(target, mbuf.shape)

    wait_all(copies)
    h2 = jnp.concatenate([hpart[j] for j in range(n)], axis=1)
    x = rms_norm(h2, ln_ref[...].reshape(1, width))
    xbuf[...] = x
    own[...] = h2.reshape(n, rows, width)
    def hidden_units(e, buf):
        load(e, 0).wait()
        u = jnp.maximum(dot_nn(xbuf[...], wi[e]), 0.0)
        hit = jnp.broadcast_to(mbuf[:, 0:1], u.shape) == e
        buf[...] = jnp.where(hit, u, 0.0).astype(BF16)

    def add_output(e, buf):
        part[...] += dot_nn(buf[...], wo[e]).reshape(part.shape)

    part[...] = jnp.zeros_like(part)
    hidden_units(0, u0)

    @pl.loop(0, experts // 2)
    def _(i):
        e = i * 2
        load(e, 1).wait()
        hidden_units(e + 1, u1)
        add_output(e, u0)
        load(e + 1, 1).wait()

        @pl.when(e + 2 < experts)
        def _():
            hidden_units(e + 2, u0)
            add_output(e + 1, u1)

        @pl.when(e + 2 >= experts)
        def _():
            add_output(e + 1, u1)

    copies = start_exchange(me, n, lambda p: part.at[p], ybuf.at[me], s5, r5)
    ybuf[me] = part[me]

    my_rows = pl.ds(pl.multiple_of(me * rows, rows), rows)
    router = jnp.concatenate([rbuf[j] for j in range(n)], axis=0)
    logits = lax.dot_general(xbuf[my_rows, :].astype(F32), router, (((1,), (1,)), ((), ())),
                             precision=lax.Precision.HIGHEST, preferred_element_type=F32)
    probs = jnp.exp(logits - jnp.max(logits, axis=-1, keepdims=True))
    probs = probs / jnp.sum(probs, axis=-1, keepdims=True)
    chosen = lax.broadcasted_iota(jnp.int32, (rows, experts), 1) == mbuf[my_rows, :][:, 0:experts]
    gate = jnp.sum(jnp.where(chosen, probs, 0.0), axis=-1, keepdims=True)
    wait_all(copies)
    y = ybuf[0]
    for j in range(1, n):
        y = y + ybuf[j]
    out_ref[...] = (own[me].astype(F32) + y.astype(BF16).astype(F32) * gate).astype(BF16)


def call(body, out_shape, in_specs, out_specs, scratch, collective=None, flops=1_000_000, moved=1_000_000, vmem=VMEM_MAX):
    params = dict(vmem_limit_bytes=vmem)
    if collective is not None:
        params.update(collective_id=collective, has_side_effects=True)
    kernel = pl.pallas_call(
        body, out_shape=out_shape, in_specs=in_specs, out_specs=out_specs, scratch_shapes=scratch,
        compiler_params=pltpu.CompilerParams(**params),
        cost_estimate=pl.CostEstimate(flops=flops, bytes_accessed=moved, transcendentals=0))

    def run(*operands):
        return kernel(*[pltpu.with_memory_space_constraint(x, pltpu.HBM) if spec is HBM_SPEC else x
                        for x, spec in zip(operands, in_specs)])
    return run


def solution(mesh):
    n = mesh.shape['ws']
    row_axes = ('dp', 'ws')
    row_vec = P(row_axes)
    row_mat = P(row_axes, None)
    cache_spec = P(row_axes, None, None, None)
    col_split = P(None, 'ws')
    in_specs = (row_mat, cache_spec, cache_spec, cache_spec, cache_spec, row_vec, row_mat, P(None, None), row_vec,
                P(None), P(None), P(None), col_split, col_split, col_split, col_split, col_split, col_split,
                col_split, P(None, None, 'ws'), P(None, 'ws', None))
    out_specs = (row_mat, cache_spec, cache_spec)
    dma = pltpu.SemaphoreType.DMA

    def decoder_block(hidden, self_k, self_v, cross_k, cross_v, positions, enc_mask, rel_bias, expert_idx,
                      ln_self, ln_cross, ln_ffn, wq_self, wk_self, wv_self, wo_self, wq_cross, wo_cross,
                      w_router, w_in, w_out):
        rows, width = hidden.shape
        heads, length = rel_bias.shape
        head_dim = width // heads
        source = enc_mask.shape[1]
        cols = wq_self.shape[1]
        experts, _, units = w_in.shape
        total = n * rows
        sds = jax.ShapeDtypeStruct

        def flat(cache):
            return jnp.swapaxes(cache, 2, 3).reshape(rows, width, cache.shape[2])

        sems = [dma((n - 1,))]
        w_tile = pltpu.VMEM((cols, width), BF16)
        ln_tile = pltpu.VMEM((width,), F32)
        q, k, v, hall, brev, lens = call(
            functools.partial(qkv_kernel, n),
            [sds((rows, width), BF16)] * 3 + [sds((total, width), BF16), sds((HEAD_PAD, length), F32), sds((rows, 128), jnp.int32)],
            [HBM_SPEC] * 7, [VMEM_SPEC] * 6,
            [pltpu.VMEM((rows, width), BF16), ln_tile, pltpu.VMEM((3, cols, width), BF16), pltpu.VMEM((heads, length), F32),
             pltpu.VMEM((rows, source), jnp.int32),
             pltpu.VMEM((n, rows, width), BF16), pltpu.VMEM((n, 3, rows, cols), BF16), pltpu.VMEM((n, 3, rows, cols), BF16)]
            + sems * 4 + [dma((7,))],
            collective=0, vmem=8 << 20,
        )(hidden, ln_self, wq_self.T, wk_self.T, wv_self.T, rel_bias, enc_mask)

        def attention_scratch(size):
            return ([pltpu.VMEM((HEAD_PAD, size), F32)] * 4
                    + [pltpu.VMEM((rows, HEAD_PAD, width), BF16), pltpu.VMEM((rows, width), F32)])

        ctx, new_k, new_v = call(
            functools.partial(self_kernel, heads),
            [sds((rows, width), BF16)] + [sds((rows, width, length), BF16)] * 2,
            [HBM_SPEC] + [VMEM_SPEC] * 4 + [HBM_SPEC] * 2, [VMEM_SPEC] + [HBM_SPEC] * 2,
            [pltpu.VMEM((rows, width, length), BF16)] * 2 + [pltpu.VMEM((width, 128), F32)] * 2
            + attention_scratch(length) + [dma((2, rows)), dma((2, rows)), pltpu.SMEM((rows,), jnp.int32), dma],
            vmem=22 << 20,
        )(positions, q, k, v, brev, flat(self_k), flat(self_v))

        qc, h1 = call(
            functools.partial(mid_kernel, n),
            [sds((rows, width), BF16), sds((total, width), BF16)],
            [VMEM_SPEC] * 2 + [HBM_SPEC] * 3, [VMEM_SPEC] * 2,
            [w_tile, ln_tile, w_tile, dma((3,)), pltpu.VMEM((n, rows, width), BF16), pltpu.VMEM((n, total, cols), BF16),
             pltpu.VMEM((n, rows, cols), BF16), pltpu.VMEM((n, rows, cols), BF16)] + sems * 6,
            collective=1, vmem=8 << 20,
        )(ctx, hall, wo_self.T, ln_cross, wq_cross.T)

        ctx2 = call(
            functools.partial(cross_kernel, heads),
            sds((rows, width), BF16),
            [SMEM_SPEC] + [VMEM_SPEC] * 2 + [HBM_SPEC] * 2, VMEM_SPEC,
            [pltpu.VMEM((rows, width, source), BF16)] * 2 + attention_scratch(source) + [dma((2, rows))],
            vmem=52 << 20,
        )(lens, qc, enc_mask, flat(cross_k), flat(cross_v))

        out = call(
            functools.partial(ffn_kernel, n),
            sds((rows, width), BF16),
            [VMEM_SPEC] * 2 + [HBM_SPEC] * 6, VMEM_SPEC,
            [pltpu.VMEM((n, rows, width), BF16), pltpu.VMEM((n, total, cols), BF16),
             pltpu.VMEM((n, experts // n, width), F32), pltpu.VMEM((n, 1, rows), jnp.int32),
             pltpu.VMEM((total, width), BF16), pltpu.VMEM((total, 128), jnp.int32),
             pltpu.VMEM((experts, width, units), BF16), pltpu.VMEM((experts, units, width), BF16),
             pltpu.VMEM((total, units), BF16), pltpu.VMEM((total, units), BF16),
             pltpu.VMEM((n, rows, width), F32), pltpu.VMEM((n, rows, width), BF16),
             pltpu.VMEM((n, rows, width), F32)]
            + sems * 10 + [dma((experts,)), dma((experts,))]
            + [w_tile, ln_tile, pltpu.VMEM((experts // n, width), F32), pltpu.VMEM((1, rows), jnp.int32), dma((4,))],
            collective=2, vmem=41 << 20,
        )(ctx2, h1, wo_cross.T, ln_ffn, w_router.T, expert_idx[None, :], w_in, w_out)

        def unflat(cache):
            return jnp.swapaxes(cache.reshape(rows, heads, head_dim, length), 2, 3)

        return out, unflat(new_k), unflat(new_v)

    return jax.shard_map(decoder_block, mesh=mesh, in_specs=in_specs, out_specs=out_specs, check_vma=False)
```

time: 105 us -> 70.7 us (0.67); the launches traced: 104 us -> 70.8 us
  Pallas kernels: 86.6 us -> 69.5 us
  local copies, waits for them, and re-layouts: 16.3 us -> 0.61 us
    pallas_call x5, Pallas kernels: 86.6 us -> 69.5 us  [run(): kernel(*[pltpu.with_memory_space_constraint(x, pltpu.HBM) if spec is HBM_...]
    unnamed x39 -> x3, local copies, waits for them, and re-layouts: 14.2 us -> 0.61 us
    broadcast_in_dim x3 -> x0, local copies, waits for them, and re-layouts: 1.28 us -> none  [the longest x1 0.7 us: decoder_block(): ln_self[None, :]]
where the time goes in v2:
time: 70.7 us; the launch traced here: 70.8 us
  Pallas kernels  69.5 us (98%)
    pallas_call x5, Pallas kernels, run(): kernel(*[pltpu.with_memory_space_constraint(x, pltpu.HBM) if spec is HBM_...  69.5 us

profile of v2, /device:TPU:0, one launch (start us, length us, event | category | flops | bytes accessed | tf_op | source)
XLA Modules:
  0.0 70.8 jit_solution(10606799105201672546)
XLA Ops:
  0.6 0.0 copy-start
  0.6 9.7 %shard_map.220 = (bf16[16,768]{1,0:T(8,128)(2,1)S(1)}, bf16[16,768]{1,0:T(8,128)(2,1)S(1)}, bf16[16,768]{1,0:T(8,128)(2,1)S(1)}, bf16[64,768]{1,0:T(8,128)(2,1)S...) custom-call(bf16[16,768]{1,0:T(8,128)(2,1)} %h_hbm.1, f32[768]{0:T(1024)} %ln_hbm.3, bf16[192,768]{1,0:T(8,128)(2,1)} %bitcast.31, ...), custom_call_target="tpu_custom_call" | custom-call | flops 1000000 | bytes 1000000 | tf_op jit(solution)/shard_map/pallas_call | solution.py:391
  10.4 13.7 %shard_map.221 = (bf16[16,768]{1,0:T(8,128)(2,1)S(1)}, bf16[16,768,384]{2,1,0:T(8,128)(2,1)}, bf16[16,768,384]{2,1,0:T(8,128)(2,1)}) custom-call(s32[16]{0:T(128)} %pos_hbm.1, bf16[16,768]{1,0:T(8,128)(2,1)S(1)} %get-tuple-element.15.q_ref, bf16[16,768]{1,0:T(8,128)(2,1)S(1)} %get-tuple-element.16.k_ref, bf16[16,768]{1,0:T(8,128)(2,1)S(1)} %get-tuple-element.17.v_ref, ...), custom_call_target="tpu_custom_call" | custom-call | flops 1000000 | bytes 1000000 | tf_op jit(solution)/shard_map/pallas_call | solution.py:391
  24.1 10.8 %shard_map.222 = (bf16[16,768]{1,0:T(8,128)(2,1)S(1)}, bf16[64,768]{1,0:T(8,128)(2,1)S(1)}) custom-call(bf16[16,768]{1,0:T(8,128)(2,1)S(1)} %get-tuple-element.19.ctx_ref, bf16[64,768]{1,0:T(8,128)(2,1)S(1)} %get-tuple-element.20.hall_ref, bf16[192,768]{1,0:T(8,128)(2,1)} %bitcast.34, f32[768]{0:T(1024)} %ln_hbm.4, bf16[192,768]{1,0:T(8,128)(2,1)} %bitcast.35), custom_call_target="tpu_custom_call" | custom-call | flops 1000000 | bytes 1000000 | tf_op jit(solution)/shard_map/pallas_call | solution.py:391
  34.9 0.0 copy-done
  34.9 13.7 %shard_map.223.ctx_ref = bf16[16,768]{1,0:T(8,128)(2,1)S(1)} custom-call(s32[16,128]{1,0:T(8,128)S(1)} %get-tuple-element.14.lens_ref, bf16[16,768]{1,0:T(8,128)(2,1)S(1)} %get-tuple-element.21.q_ref, s32[16,1024]{1,0:T(8,128)S(1)} %copy-done, bf16[16,768,1024]{2,1,0:T(8,128)(2,1)} %bitcast.26, bf16[16,768,1024]{2,1,0:T(8,128)(2,1)} %bitcast.27), custom_call_target="tpu_custom_call" | custom-call | flops 1000000 | bytes 1000000 | tf_op jit(solution)/shard_map/pallas_call | solution.py:391
  48.7 21.5 %shard_map.224 = bf16[16,768]{1,0:T(8,128)(2,1)S(1)} custom-call(bf16[16,768]{1,0:T(8,128)(2,1)S(1)} %shard_map.223.ctx_ref, bf16[64,768]{1,0:T(8,128)(2,1)S(1)} %get-tuple-element.22.h1_ref, bf16[192,768]{1,0:T(8,128)(2,1)} %bitcast.30, f32[768]{0:T(1024)} %ln_hbm.5, f32[4,768]{1,0:T(4,128)} %bitcast.36, s32[1,16]{1,0:T(1,128)} %bitcast.37, ...), custom_call_target="tpu_custom_call" | custom-call | flops 1000000 | bytes 1000000 | tf_op jit(solution)/shard_map/pallas_call | solution.py:391
  70.2 0.6 copy.25
Async XLA Ops:
  0.6 34.3 %copy-start = (s32[16,1024]{1,0:T(8,128)S(1)}, s32[16,1024]{1,0:T(8,128)}, u32[]{:S(2)}) copy-start(s32[16,1024]{1,0:T(8,128)} %mask_ref.1) | copy-start | bytes 196612

commit v3 on v2

--- a/solution.py
+++ b/solution.py
@@ -70,14 +70,35 @@
     return copies
 
 
-def qkv_kernel(n, h_hbm, ln_hbm, wq_hbm, wk_hbm, wv_hbm, bias_hbm, mask_hbm,
-               q_ref, k_ref, v_ref, hall_ref, brev_ref, lens_ref,
-               h_ref, ln_ref, w_ref, bias_ref, mask_ref, hbuf, sendbuf, recvbuf, s1, r1, s2, r2, in_sem):
+def read_rows(pairs, sem):
+    def copy(i, r):
+        return pltpu.make_async_copy(pairs[i][0].at[r], pairs[i][1].at[r], sem.at[i, r])
+    rows = pairs[0][1].shape[0]
+
+    def start():
+        @pl.loop(0, rows)
+        def _(r):
+            for i in range(len(pairs)):
+                copy(i, r).start()
+
+    def wait():
+        @pl.loop(0, rows)
+        def _(r):
+            for i in range(len(pairs)):
+                copy(i, r).wait()
+    return start, wait
+
+
+def qkv_kernel(n, h_hbm, ln_hbm, wq_hbm, wk_hbm, wv_hbm, bias_hbm, mask_hbm, sk_hbm, sv_hbm,
+               q_ref, k_ref, v_ref, hall_ref, brev_ref, lens_ref, sk_ref, sv_ref,
+               h_ref, ln_ref, w_ref, bias_ref, mask_ref, hbuf, sendbuf, recvbuf, s1, r1, s2, r2, in_sem, row_sem):
     me = lax.axis_index("ws")
     rows, width = h_ref.shape
     cols = w_ref.shape[1]
     loads = fetch([(h_hbm, h_ref), (ln_hbm, ln_ref), (bias_hbm, bias_ref), (mask_hbm, mask_ref)]
                   + [(w, w_ref.at[i]) for i, w in enumerate((wq_hbm, wk_hbm, wv_hbm))], in_sem)
+    start_rows, wait_rows = read_rows([(sk_hbm, sk_ref), (sv_hbm, sv_ref)], row_sem)
+    start_rows()
     entry_barrier(me, n)
     loads[0].wait()
     copies = start_exchange(me, n, lambda p: h_ref, hbuf.at[me], s1, r1)
@@ -102,6 +123,7 @@
     wait_all(copies)
     for i, o in enumerate((q_ref, k_ref, v_ref)):
         o[...] = jnp.concatenate([recvbuf[j, i] for j in range(n)], axis=1)
+    wait_rows()
 
 
 def head_mask(shape, head_dim):
@@ -129,7 +151,7 @@
         total = None
         for t in range(length // 128):
             lanes = slice(t * 128, (t + 1) * 128)
-            term = value[h * head_dim:(h + 1) * head_dim, lanes].astype(F32) * prob[h:h + 1, lanes]
+            term = value(slice(h * head_dim, (h + 1) * head_dim), t).astype(F32) * prob[h:h + 1, lanes]
             total = term if total is None else total + term
         parts.append(total)
     return jnp.sum(jnp.transpose(jnp.concatenate(parts, axis=0)), axis=0, keepdims=True)
@@ -137,77 +159,85 @@
 
 def self_kernel(heads, pos_hbm, q_ref, k_ref, v_ref, brev_ref, sk_ref, sv_ref,
                 ctx_ref, nk_ref, nv_ref,
-                kbuf, vbuf, kt, vt, s0, s1, p0, p1, qblk, cf, in_sem, out_sem, pos_ref, pos_sem):
-    rows, width, length = kbuf.shape
+                ktile, vtile, kt, vt, s0, s1, p0, p1, qblk, cf, xf, snew, out_sem, pos_ref, pos_sem):
+    rows, width, length = sk_ref.shape
     head_dim = width // heads
+    tiles = length // 128
     scalars = pltpu.make_async_copy(pos_hbm, pos_ref, pos_sem)
     scalars.start()
-
-    def load(r, i):
-        src, buf = ((sk_ref, kbuf), (sv_ref, vbuf))[i]
-        return pltpu.make_async_copy(src.at[r], buf.at[r], in_sem.at[i, r])
-
-    def save(r, i):
-        buf, dst = ((kbuf, nk_ref), (vbuf, nv_ref))[i]
-        return pltpu.make_async_copy(buf.at[r], dst.at[r], out_sem.at[i, r])
-
-    for r in range(rows):
-        load(r, 0).start()
-        load(r, 1).start()
 
     pad = jnp.zeros((128 - rows, width), F32)
     kt[...] = jnp.transpose(jnp.concatenate([k_ref[...].astype(F32), pad], axis=0))
     vt[...] = jnp.transpose(jnp.concatenate([v_ref[...].astype(F32), pad], axis=0))
     spread_heads(q_ref, qblk, head_dim)
+    snew[...] = dot_nn(qblk[...].reshape(rows * HEAD_PAD, width), kt[...].astype(BF16)).reshape(snew.shape)
     sbufs, pbufs = (s0, s1), (p0, p1)
     scalars.wait()
 
-    def insert(r, buf, cols):
+    def insert(r, cache, tile_buf, cols):
         pos = pos_ref[r]
         tile = pos // 128
         at = pos - tile * 128
         new = jnp.broadcast_to(cols[:, r:r + 1], (width, 128))
-        view = buf.at[r, :, pl.ds(pl.multiple_of(tile * 128, 128), 128)]
+        old = cache[r, :, pl.ds(pl.multiple_of(tile * 128, 128), 128)]
         hit = lax.broadcasted_iota(jnp.int32, (width, 128), 1) == at
-        view[...] = jnp.where(hit, new, view[...].astype(F32)).astype(BF16)
+        tile_buf[r] = jnp.where(hit, new, old.astype(F32)).astype(BF16)
+
+    def save(r):
+        tile = pos_ref[r] // 128
+        for i, (cache, tile_buf, dst) in enumerate(((sk_ref, ktile, nk_ref), (sv_ref, vtile, nv_ref))):
+            for t in range(tiles):
+                lanes = slice(t * 128, (t + 1) * 128)
+
+                @pl.when(tile == t)
+                def _():
+                    pltpu.make_async_copy(tile_buf.at[r], dst.at[r, :, lanes], out_sem.at[i, r]).start()
+
+                @pl.when(tile != t)
+                def _():
+                    pltpu.make_async_copy(cache.at[r, :, lanes], dst.at[r, :, lanes], out_sem.at[i, r]).start()
 
     def softmax(r):
         pos = pos_ref[r]
         bias = pltpu.roll(brev_ref[...], lax.rem(pos + 1, length), 1)
         lane = lax.broadcasted_iota(jnp.int32, (HEAD_PAD, length), 1)
-        pbufs[r % 2][...] = softmax_rows(jnp.where(lane <= pos, sbufs[r % 2][...] + bias, NEG_BIG))
-
-    for step in range(rows + 3):
-        r = step
-        if r < rows:
-            load(r, 0).wait()
-            load(r, 1).wait()
-        if step >= 3:
-            done = step - 3
-            cf[done:done + 1, :] = weighted_values(pbufs[done % 2], vbuf.at[done], heads, head_dim, length)
-        if 2 <= step < rows + 2:
-            softmax(step - 2)
+        pick = lax.broadcasted_iota(jnp.int32, (HEAD_PAD, 128), 1) == r
+        fresh = jnp.sum(jnp.where(pick, snew[r], 0.0), axis=-1, keepdims=True)
+        scores = jnp.where(lane == pos, fresh, sbufs[r % 2][...]) + bias
+        prob = softmax_rows(jnp.where(lane <= pos, scores, NEG_BIG))
+        pbufs[r % 2][...] = jnp.where(lane == pos, 0.0, prob)
+        at_pos = jnp.sum(jnp.where(lane == pos, prob, 0.0), axis=-1, keepdims=True)
+        spread = jnp.where(head_mask((HEAD_PAD, width), head_dim), jnp.broadcast_to(at_pos, (HEAD_PAD, width)), 0.0)
+        xf[r:r + 1, :] = jnp.sum(spread, axis=0, keepdims=True) * v_ref[r:r + 1, :].astype(F32)
+
+    for step in range(rows + 2):
+        if step >= 2:
+            done = step - 2
+            cf[done:done + 1, :] = xf[done:done + 1, :] + weighted_values(
+                pbufs[done % 2], lambda d, t: sv_ref[done, d, t * 128:(t + 1) * 128], heads, head_dim, length)
         if 1 <= step < rows + 1:
-            sbufs[(step - 1) % 2][...] = dot_nn(qblk[step - 1], kbuf[step - 1])
-        if r < rows:
-            insert(r, kbuf, kt)
-            insert(r, vbuf, vt)
-        if 1 <= step < rows + 1:
-            save(step - 1, 0).start()
-            save(step - 1, 1).start()
+            softmax(step - 1)
+            save(step - 1)
+        if step < rows:
+            sbufs[step % 2][...] = dot_nn(qblk[step], sk_ref[step])
+            insert(step, sk_ref, ktile, kt)
+            insert(step, sv_ref, vtile, vt)
 
     ctx_ref[...] = cf[...].astype(BF16)
     for r in range(rows):
-        save(r, 0).wait()
-        save(r, 1).wait()
-
-
-def mid_kernel(n, ctx_ref, hall_ref, wo_hbm, ln_hbm, wq_hbm,
-               q_ref, h1_ref, wo_ref, ln_ref, wq_ref, in_sem, cbuf, hpart, sendbuf, recvbuf, s1, r1, s2, r2, s3, r3):
+        pltpu.make_async_copy(sk_ref.at[r], nk_ref.at[r], out_sem.at[0, r]).wait()
+        pltpu.make_async_copy(sv_ref.at[r], nv_ref.at[r], out_sem.at[1, r]).wait()
+
+
+def mid_kernel(n, ctx_ref, hall_ref, wo_hbm, ln_hbm, wq_hbm, ck_hbm, cv_hbm,
+               q_ref, h1_ref, ck_ref, cv_ref, wo_ref, ln_ref, wq_ref, in_sem, row_sem, cbuf, hpart, sendbuf, recvbuf, s1, r1, s2, r2, s3, r3):
     me = lax.axis_index("ws")
     rows, width = ctx_ref.shape
     cols = wo_ref.shape[0]
     loads = fetch([(wo_hbm, wo_ref), (ln_hbm, ln_ref), (wq_hbm, wq_ref)], in_sem)
+    near = ck_ref.shape[2]
+    start_rows, wait_rows = read_rows([(ck_hbm.at[:, :, 0:near], ck_ref), (cv_hbm.at[:, :, 0:near], cv_ref)], row_sem)
+    start_rows()
     entry_barrier(me, n)
     copies = start_exchange(me, n, lambda p: ctx_ref, cbuf.at[me], s1, r1)
     cbuf[me] = ctx_ref[...]
@@ -226,57 +256,101 @@
     recvbuf[me] = sendbuf[me]
     wait_all(copies)
     q_ref[...] = jnp.concatenate([recvbuf[j] for j in range(n)], axis=1)
-
-
-def cross_kernel(heads, lens_ref, q_ref, mask_ref, ck_ref, cv_ref,
+    wait_rows()
+
+
+def cross_kernel(heads, lens_ref, q_ref, mask_ref, kn_ref, vn_ref, ck_ref, cv_ref,
                  ctx_ref, kbuf, vbuf, s0, s1, p0, p1, qblk, cf, in_sem):
-    rows, width, length = kbuf.shape
+    rows, width, near = kn_ref.shape
+    length = near + kbuf.shape[2]
     head_dim = width // heads
-    tiles = length // 128
+    block = 256
+    tiles, near_tiles = length // 128, near // 128
 
     def tile_count(r):
         return (lens_ref[r, 0] + 127) // 128
 
-    def per_size(r, body):
+    def far_copies(r, body):
         count = tile_count(r)
-        for t in range(1, tiles + 1):
+        for t in range(near_tiles + 1, tiles + 1):
             @pl.when(count == t)
-            def _(t=t):
-                body(t * 128)
-
-    def load(r, i, size):
-        src, buf = ((ck_ref, kbuf), (cv_ref, vbuf))[i]
-        return pltpu.make_async_copy(src.at[r, :, 0:size], buf.at[r, :, 0:size], in_sem.at[i, r])
+            def _(size=(t - near_tiles) * 128):
+                body(lambda i: pltpu.make_async_copy(
+                    (ck_ref, cv_ref)[i].at[r, :, near:near + size], (kbuf, vbuf)[i].at[r, :, 0:size], in_sem.at[i, r]))
+
+    def per_block(r, body):
+        blocks = (lens_ref[r, 0] + block - 1) // block
+        for t in range(1, length // block + 1):
+            @pl.when(blocks == t)
+            def _(size=t * block):
+                body(size)
 
     @pl.loop(0, rows)
     def _(r):
-        per_size(r, lambda size: load(r, 0, size).start())
-        per_size(r, lambda size: load(r, 1, size).start())
+        far_copies(r, lambda copy: (copy(0).start(), copy(1).start()))
 
     spread_heads(q_ref, qblk, head_dim)
 
     @pl.loop(0, rows)
     def _(r):
-        @pl.loop(tile_count(r), tiles)
-        def _(t):
-            vbuf[r, :, pl.ds(pl.multiple_of(t * 128, 128), 128)] = jnp.zeros((width, 128), BF16)
-
-    sbufs, pbufs = (s0, s1), (p0, p1)
-
-    for step in range(rows + 2):
-        if step < rows:
-            per_size(step, lambda size: load(step, 0, size).wait())
-        if step >= 2:
-            per_size(step - 2, lambda size: load(step - 2, 1, size).wait())
-            done = step - 2
-            cf[done:done + 1, :] = weighted_values(pbufs[done % 2], vbuf.at[done], heads, head_dim, length)
-        if 1 <= step < rows + 1:
-            r = step - 1
-            keep = jnp.broadcast_to(mask_ref[r:r + 1, :], (HEAD_PAD, length)) == 1
-            pbufs[r % 2][...] = softmax_rows(jnp.where(keep, sbufs[r % 2][...], NEG_BIG))
-        if step < rows:
-            sbufs[step % 2][...] = dot_nn(qblk[step], kbuf[step])
-
+        for t in range(near_tiles + 1, tiles, 2):
+            @pl.when(tile_count(r) == t)
+            def _(at=(t - near_tiles) * 128):
+                vbuf[r, :, at:at + 128] = jnp.zeros((width, 128), BF16)
+
+    def scores(r, size, out):
+        first = min(size, near)
+        out[:, 0:first] = dot_nn(qblk[r], kn_ref[r, :, 0:first])
+        if size > near:
+            out[:, near:size] = dot_nn(qblk[r], kbuf[r, :, 0:size - near])
+
+    def softmax(r, src, out):
+        keep = jnp.broadcast_to(mask_ref[pl.ds(r, 1), :], (HEAD_PAD, length)) == 1
+        out[...] = softmax_rows(jnp.where(keep, src[...], NEG_BIG))
+
+    def values(r, size, prob):
+        def tile(d, t):
+            if t < near_tiles:
+                return vn_ref[r, d, t * 128:(t + 1) * 128]
+            return vbuf[r, d, (t - near_tiles) * 128:(t - near_tiles + 1) * 128]
+        cf[pl.ds(r, 1), :] = weighted_values(prob, tile, heads, head_dim, size)
+
+    def arrived(r, i):
+        far_copies(r, lambda copy: copy(i).wait())
+
+    arrived(0, 0)
+    per_block(0, lambda size: scores(0, size, s0))
+    arrived(1, 0)
+
+    def second(size):
+        softmax(0, s0, p0)
+        scores(1, size, s1)
+    per_block(1, second)
+
+    def step(r, sa, sb, pa, pb):
+        arrived(r, 1)
+        arrived(r + 2, 0)
+
+        def outer(size_v):
+            def inner(size_s):
+                values(r, size_v, pa)
+                softmax(r + 1, sb, pb)
+                scores(r + 2, size_s, sa)
+            per_block(r + 2, inner)
+        per_block(r, outer)
+
+    @pl.loop(0, (rows - 2) // 2)
+    def _(i):
+        step(2 * i, s0, s1, p0, p1)
+        step(2 * i + 1, s1, s0, p1, p0)
+
+    def last_but_one(size):
+        values(rows - 2, size, p0)
+        softmax(rows - 1, s1, p1)
+    arrived(rows - 2, 1)
+    per_block(rows - 2, last_but_one)
+    arrived(rows - 1, 1)
+    per_block(rows - 1, lambda size: values(rows - 1, size, p1))
     ctx_ref[...] = cf[...].astype(BF16)
 
 
@@ -424,16 +498,18 @@
         sems = [dma((n - 1,))]
         w_tile = pltpu.VMEM((cols, width), BF16)
         ln_tile = pltpu.VMEM((width,), F32)
-        q, k, v, hall, brev, lens = call(
+        near = source // 2
+        q, k, v, hall, brev, lens, near_sk, near_sv = call(
             functools.partial(qkv_kernel, n),
-            [sds((rows, width), BF16)] * 3 + [sds((total, width), BF16), sds((HEAD_PAD, length), F32), sds((rows, 128), jnp.int32)],
-            [HBM_SPEC] * 7, [VMEM_SPEC] * 6,
+            [sds((rows, width), BF16)] * 3 + [sds((total, width), BF16), sds((HEAD_PAD, length), F32), sds((rows, 128), jnp.int32)]
+            + [sds((rows, width, length), BF16)] * 2,
+            [HBM_SPEC] * 9, [VMEM_SPEC] * 8,
             [pltpu.VMEM((rows, width), BF16), ln_tile, pltpu.VMEM((3, cols, width), BF16), pltpu.VMEM((heads, length), F32),
              pltpu.VMEM((rows, source), jnp.int32),
              pltpu.VMEM((n, rows, width), BF16), pltpu.VMEM((n, 3, rows, cols), BF16), pltpu.VMEM((n, 3, rows, cols), BF16)]
-            + sems * 4 + [dma((7,))],
+            + sems * 4 + [dma((7,)), dma((2, rows))],
             collective=0, vmem=8 << 20,
-        )(hidden, ln_self, wq_self.T, wk_self.T, wv_self.T, rel_bias, enc_mask)
+        )(hidden, ln_self, wq_self.T, wk_self.T, wv_self.T, rel_bias, enc_mask, flat(self_k), flat(self_v))
 
         def attention_scratch(size):
             return ([pltpu.VMEM((HEAD_PAD, size), F32)] * 4
@@ -442,28 +518,29 @@
         ctx, new_k, new_v = call(
             functools.partial(self_kernel, heads),
             [sds((rows, width), BF16)] + [sds((rows, width, length), BF16)] * 2,
-            [HBM_SPEC] + [VMEM_SPEC] * 4 + [HBM_SPEC] * 2, [VMEM_SPEC] + [HBM_SPEC] * 2,
-            [pltpu.VMEM((rows, width, length), BF16)] * 2 + [pltpu.VMEM((width, 128), F32)] * 2
-            + attention_scratch(length) + [dma((2, rows)), dma((2, rows)), pltpu.SMEM((rows,), jnp.int32), dma],
-            vmem=22 << 20,
-        )(positions, q, k, v, brev, flat(self_k), flat(self_v))
-
-        qc, h1 = call(
+            [HBM_SPEC] + [VMEM_SPEC] * 6, [VMEM_SPEC] + [HBM_SPEC] * 2,
+            [pltpu.VMEM((rows, width, 128), BF16)] * 2 + [pltpu.VMEM((width, 128), F32)] * 2 + attention_scratch(length)
+            + [pltpu.VMEM((rows, width), F32), pltpu.VMEM((rows, HEAD_PAD, 128), F32),
+               dma((2, rows)), pltpu.SMEM((rows,), jnp.int32), dma],
+            vmem=12 << 20,
+        )(positions, q, k, v, brev, near_sk, near_sv)
+
+        qc, h1, near_ck, near_cv = call(
             functools.partial(mid_kernel, n),
-            [sds((rows, width), BF16), sds((total, width), BF16)],
-            [VMEM_SPEC] * 2 + [HBM_SPEC] * 3, [VMEM_SPEC] * 2,
-            [w_tile, ln_tile, w_tile, dma((3,)), pltpu.VMEM((n, rows, width), BF16), pltpu.VMEM((n, total, cols), BF16),
+            [sds((rows, width), BF16), sds((total, width), BF16)] + [sds((rows, width, near), BF16)] * 2,
+            [VMEM_SPEC] * 2 + [HBM_SPEC] * 5, [VMEM_SPEC] * 4,
+            [w_tile, ln_tile, w_tile, dma((3,)), dma((2, rows)), pltpu.VMEM((n, rows, width), BF16), pltpu.VMEM((n, total, cols), BF16),
              pltpu.VMEM((n, rows, cols), BF16), pltpu.VMEM((n, rows, cols), BF16)] + sems * 6,
             collective=1, vmem=8 << 20,
-        )(ctx, hall, wo_self.T, ln_cross, wq_cross.T)
+        )(ctx, hall, wo_self.T, ln_cross, wq_cross.T, flat(cross_k), flat(cross_v))
 
         ctx2 = call(
             functools.partial(cross_kernel, heads),
             sds((rows, width), BF16),
-            [SMEM_SPEC] + [VMEM_SPEC] * 2 + [HBM_SPEC] * 2, VMEM_SPEC,
-            [pltpu.VMEM((rows, width, source), BF16)] * 2 + attention_scratch(source) + [dma((2, rows))],
-            vmem=52 << 20,
-        )(lens, qc, enc_mask, flat(cross_k), flat(cross_v))
+            [SMEM_SPEC] + [VMEM_SPEC] * 4 + [HBM_SPEC] * 2, VMEM_SPEC,
+            [pltpu.VMEM((rows, width, source - near), BF16)] * 2 + attention_scratch(source) + [dma((2, rows))],
+            vmem=26 << 20,
+        )(lens, qc, enc_mask, near_ck, near_cv, flat(cross_k), flat(cross_v))
 
         out = call(
             functools.partial(ffn_kernel, n),

time: 70.7 us -> 62.1 us (0.88)
  Pallas kernels: 69.5 us -> 60.7 us
    pallas_call x5, Pallas kernels: 69.5 us -> 60.7 us  [run(): kernel(*[pltpu.with_memory_space_constraint(x, pltpu.HBM) if spec is HBM_...]
where the time goes in v3:
time: 62.1 us
  Pallas kernels  60.7 us (98%)
  between operations  0.69 us (1%)
    pallas_call x5, Pallas kernels, run(): kernel(*[pltpu.with_memory_space_constraint(x, pltpu.HBM) if spec is HBM_...  60.7 us

profile of v3, /device:TPU:0, one launch (start us, length us, event | category | flops | bytes accessed | tf_op | source)
XLA Modules:
  0.0 62.1 jit_solution(5141005386937699593)
XLA Ops:
  0.6 10.3 %shard_map.220 = (bf16[16,768]{1,0:T(8,128)(2,1)S(1)}, bf16[16,768]{1,0:T(8,128)(2,1)S(1)}, bf16[16,768]{1,0:T(8,128)(2,1)S(1)}, bf16[64,768]{1,0:T(8,128)(2,1)S...) custom-call(bf16[16,768]{1,0:T(8,128)(2,1)} %h_hbm.1, ...), custom_call_target="tpu_custom_call" | custom-call | flops 1000000 | bytes 1000000 | tf_op jit(solution)/shard_map/pallas_call | solution.py:465
  10.9 8.8 %shard_map.221 = (bf16[16,768]{1,0:T(8,128)(2,1)S(1)}, bf16[16,768,384]{2,1,0:T(8,128)(2,1)}, bf16[16,768,384]{2,1,0:T(8,128)(2,1)}) custom-call(s32[16]{0:T(128)} %pos_hbm.1, bf16[16,768]{1,0:T(8,128)(2,1)S(1)} %get-tuple-element.19.q_ref, bf16[16,768]{1,0:T(8,128)(2,1)S(1)} %get-tuple-element.20.k_ref, bf16[16,768]{1,0:T(8,128)(2,1)S(1)} %get-tuple-element.21.v_ref, ...), custom_call_target="tpu_custom_call" | custom-call | flops 1000000 | bytes 1000000 | tf_op jit(solution)/shard_map/pallas_call | solution.py:465
  19.7 0.0 copy-start
  19.7 11.2 %shard_map.222 = (bf16[16,768]{1,0:T(8,128)(2,1)S(1)}, bf16[64,768]{1,0:T(8,128)(2,1)S(1)}, bf16[16,768,512]{2,1,0:T(8,128)(2,1)S(1)}, bf16[16,768,512]{2,1,0:T(8,128)(2,1)S(1)}) custom-call(bf16[16,768]{1,0:T(8,128)(2,1)S(1)} %get-tuple-element.25.ctx_ref, bf16[64,768]{1,0:T(8,128)(2,1)S(1)} %get-tuple-element.26.hall_ref, bf16[192,768]{1,0:T(8,128)(2,1)} %bitcast.32, ...), custom_call_target="tpu_custom_call" | custom-call | flops 1000000 | bytes 1000000 | tf_op jit(solution)/shard_map/pallas_call | solution.py:465
  30.9 0.0 copy-done
  30.9 9.0 %shard_map.223.ctx_ref = bf16[16,768]{1,0:T(8,128)(2,1)S(1)} custom-call(s32[16,128]{1,0:T(8,128)S(1)} %get-tuple-element.18.lens_ref, bf16[16,768]{1,0:T(8,128)(2,1)S(1)} %get-tuple-element.27.q_ref, s32[16,1024]{1,0:T(8,128)S(1)} %copy-done, bf16[16,768,512]{2,1,0:T(8,128)(2,1)S(1)} %get-tuple-element.28.kn_ref, ...), custom_call_target="tpu_custom_call" | custom-call | flops 1000000 | bytes 1000000 | tf_op jit(solution)/shard_map/pallas_call | solution.py:465
  39.9 21.5 %shard_map.224 = bf16[16,768]{1,0:T(8,128)(2,1)S(1)} custom-call(bf16[16,768]{1,0:T(8,128)(2,1)S(1)} %shard_map.223.ctx_ref, bf16[64,768]{1,0:T(8,128)(2,1)S(1)} %get-tuple-element.30.h1_ref, bf16[192,768]{1,0:T(8,128)(2,1)} %bitcast.34, f32[768]{0:T(1024)} %ln_hbm.5, f32[4,768]{1,0:T(4,128)} %bitcast.38, s32[1,16]{1,0:T(1,128)} %bitcast.39, ...), custom_call_target="tpu_custom_call" | custom-call | flops 1000000 | bytes 1000000 | tf_op jit(solution)/shard_map/pallas_call | solution.py:465
  61.4 0.6 copy.25
Async XLA Ops:
  19.7 11.2 %copy-start = (s32[16,1024]{1,0:T(8,128)S(1)}, s32[16,1024]{1,0:T(8,128)}, u32[]{:S(2)}) copy-start(s32[16,1024]{1,0:T(8,128)} %mask_ref.1) | copy-start | bytes 196612

commit v4 on v3

--- a/solution.py
+++ b/solution.py
@@ -16,6 +16,8 @@
 HBM_SPEC = pl.BlockSpec(memory_space=pltpu.HBM)
 VMEM_MAX = 67_000_000
 HEAD_PAD = 16
+NEAR, SLOTS, EARLY = 512, 8, 4
+VM3, VM4, VM5 = 8, 14, 39
 
 
 def rms_norm(hidden, scale):
@@ -32,11 +34,20 @@
     return lax.dot_general(a, b, (((1,), (1,)), ((), ())), preferred_element_type=F32)
 
 
-def entry_barrier(me, n):
+def entry_barrier(me, n, across=None):
     sem = pltpu.get_barrier_semaphore()
     for k in range(1, n):
         pl.semaphore_signal(sem, inc=1, device_id={"ws": lax.rem(me + k, n)}, device_id_type=MESH)
-    pl.semaphore_wait(sem, n - 1)
+    if across is not None:
+        pl.semaphore_signal(sem, inc=1, device_id=across, device_id_type=MESH)
+    pl.semaphore_wait(sem, n - 1 if across is None else n)
+
+
+def send(src, dst, send_sem, recv_sem, device):
+    copy = pltpu.make_async_remote_copy(src_ref=src, dst_ref=dst, send_sem=send_sem, recv_sem=recv_sem,
+                                        device_id=device, device_id_type=MESH)
+    copy.start()
+    return copy
 
 
 def start_exchange(me, n, src_of, dst, send_sem, recv_sem):
@@ -89,13 +100,16 @@
     return start, wait
 
 
-def qkv_kernel(n, h_hbm, ln_hbm, wq_hbm, wk_hbm, wv_hbm, bias_hbm, mask_hbm, sk_hbm, sv_hbm,
-               q_ref, k_ref, v_ref, hall_ref, brev_ref, lens_ref, sk_ref, sv_ref,
-               h_ref, ln_ref, w_ref, bias_ref, mask_ref, hbuf, sendbuf, recvbuf, s1, r1, s2, r2, in_sem, row_sem):
+def qkv_kernel(n, h_hbm, ln_hbm, wq_hbm, wk_hbm, wv_hbm, bias_hbm, mask_hbm, wc_hbm, sk_hbm, sv_hbm,
+               q_ref, k_ref, v_ref, hall_ref, brev_ref, lens_ref, wc_half, sk_ref, sv_ref,
+               h_ref, ln_ref, w_ref, bias_ref, mask_ref, hbuf, sendbuf, recvbuf, s1, r1, s2, r2, in_sem, row_sem,
+               wc_own, swc, rwc):
     me = lax.axis_index("ws")
     rows, width = h_ref.shape
     cols = w_ref.shape[1]
-    loads = fetch([(h_hbm, h_ref), (ln_hbm, ln_ref), (bias_hbm, bias_ref), (mask_hbm, mask_ref)]
+    half = cols // 2
+    start = pl.multiple_of(lax.axis_index("dp") * half, 16)
+    loads = fetch([(h_hbm, h_ref), (wc_hbm.at[pl.ds(start, half)], wc_own), (ln_hbm, ln_ref), (bias_hbm, bias_ref), (mask_hbm, mask_ref)]
                   + [(w, w_ref.at[i]) for i, w in enumerate((wq_hbm, wk_hbm, wv_hbm))], in_sem)
     start_rows, wait_rows = read_rows([(sk_hbm, sk_ref), (sv_hbm, sv_ref)], row_sem)
     start_rows()
@@ -103,7 +117,11 @@
     loads[0].wait()
     copies = start_exchange(me, n, lambda p: h_ref, hbuf.at[me], s1, r1)
     hbuf[me] = h_ref[...]
-    for load in loads[1:]:
+    other = {"ws": lax.rem(me + n // 2, n)}
+    loads[1].wait()
+    cut = 80
+    bulk = [send(wc_own.at[0:cut], wc_half.at[0:cut], swc.at[0], rwc.at[0], other)]
+    for load in loads[2:]:
         load.wait()
     lens_ref[...] = jnp.broadcast_to(jnp.sum(mask_ref[...], axis=1, keepdims=True), lens_ref.shape)
     heads, length = bias_ref.shape
@@ -119,10 +137,12 @@
     for i in range(3):
         sendbuf[:, i] = dot_nt(x, w_ref[i]).astype(BF16).reshape(n, rows, cols)
     copies = start_exchange(me, n, lambda p: sendbuf.at[p], recvbuf.at[me], s2, r2)
+    bulk.append(send(wc_own.at[cut:half], wc_half.at[cut:half], swc.at[1], rwc.at[1], other))
     recvbuf[me] = sendbuf[me]
     wait_all(copies)
     for i, o in enumerate((q_ref, k_ref, v_ref)):
         o[...] = jnp.concatenate([recvbuf[j, i] for j in range(n)], axis=1)
+    wait_all(bulk)
     wait_rows()
 
 
@@ -229,20 +249,33 @@
         pltpu.make_async_copy(sv_ref.at[r], nv_ref.at[r], out_sem.at[1, r]).wait()
 
 
-def mid_kernel(n, ctx_ref, hall_ref, wo_hbm, ln_hbm, wq_hbm, ck_hbm, cv_hbm,
-               q_ref, h1_ref, ck_ref, cv_ref, wo_ref, ln_ref, wq_ref, in_sem, row_sem, cbuf, hpart, sendbuf, recvbuf, s1, r1, s2, r2, s3, r3):
+def mid_kernel(n, ctx_ref, hall_ref, wo_hbm, ln_hbm, wq_hbm, wr_hbm, idx_hbm, wc_half, wc_hbm, ck_hbm, cv_hbm, win_hbm,
+               q_ref, h1_ref, wr_ref, idx_ref, wc_ref, ck_ref, cv_ref, win_ref, wr_own, idx_own, sr, rr, si, ri, wc_own, sw, rw, wo_ref, ln_ref, wq_ref, in_sem, row_sem, win_sem, cbuf, hpart, sendbuf, recvbuf, s1, r1, s2, r2, s3, r3):
     me = lax.axis_index("ws")
     rows, width = ctx_ref.shape
     cols = wo_ref.shape[0]
-    loads = fetch([(wo_hbm, wo_ref), (ln_hbm, ln_ref), (wq_hbm, wq_ref)], in_sem)
+    loads = fetch([(wo_hbm, wo_ref), (ln_hbm, ln_ref), (wq_hbm, wq_ref), (wr_hbm, wr_own), (idx_hbm, idx_own), (wc_hbm, wc_own)], in_sem)
     near = ck_ref.shape[2]
     start_rows, wait_rows = read_rows([(ck_hbm.at[:, :, 0:near], ck_ref), (cv_hbm.at[:, :, 0:near], cv_ref)], row_sem)
+    start_win, wait_win = read_rows([(win_hbm, win_ref)], win_sem)
     start_rows()
-    entry_barrier(me, n)
+    start_win()
+    group = lax.axis_index("dp")
+    facing, sibling = lax.rem(me + n // 2, n), me + 1 - 2 * lax.rem(me, 2)
+    half = cols // 2
+    mine_half = pl.ds(pl.multiple_of(group * half, 16), half)
+    its_half = pl.ds(pl.multiple_of((1 - group) * half, 16), half)
+    across = {"dp": 1 - group, "ws": me}
+    entry_barrier(me, n, across)
     copies = start_exchange(me, n, lambda p: ctx_ref, cbuf.at[me], s1, r1)
+    swap = send(wc_half, wc_ref.at[facing, mine_half], sw.at[0], rw.at[0], across)
+    bulk = [send(wc_half, wc_ref.at[facing, mine_half], sw.at[1], rw.at[1], {"ws": sibling})]
     cbuf[me] = ctx_ref[...]
     mine = my_columns(hall_ref[...].astype(F32), me, n, cols)
     wait_all(loads)
+    bulk.append(send(wc_own, wc_ref.at[me], sw.at[2], rw.at[2], {"ws": sibling}))
+    wc_ref[me] = wc_own[...]
+    wc_ref[facing, mine_half] = wc_half[...]
     wait_all(copies)
     attn = dot_nt(cbuf[...].reshape(n * rows, width), wo_ref[...])
     hpart[me] = (mine + attn).astype(BF16)
@@ -252,20 +285,32 @@
     h1_ref[...] = h1
     x = rms_norm(h1, ln_ref[...].reshape(1, width))
     sendbuf[...] = dot_nt(x, wq_ref[...]).astype(BF16).reshape(n, rows, cols)
-    copies = start_exchange(me, n, lambda p: sendbuf.at[p], recvbuf.at[me], s3, r3)
+    copies = (start_exchange(me, n, lambda p: sendbuf.at[p], recvbuf.at[me], s3, r3)
+              + start_exchange(me, n, lambda p: wr_own, wr_ref.at[me], sr, rr)
+              + start_exchange(me, n, lambda p: idx_own, idx_ref.at[me], si, ri))
     recvbuf[me] = sendbuf[me]
+    wr_ref[me] = wr_own[...]
+    idx_ref[me] = idx_own[...]
+    swap.wait()
+    bulk.append(send(wc_ref.at[facing, its_half], wc_ref.at[facing, its_half], sw.at[3], rw.at[3], {"ws": sibling}))
     wait_all(copies)
     q_ref[...] = jnp.concatenate([recvbuf[j] for j in range(n)], axis=1)
+    wait_all(bulk)
     wait_rows()
+    wait_win()
 
 
 def cross_kernel(heads, lens_ref, q_ref, mask_ref, kn_ref, vn_ref, ck_ref, cv_ref,
                  ctx_ref, kbuf, vbuf, s0, s1, p0, p1, qblk, cf, in_sem):
     rows, width, near = kn_ref.shape
+    slots = kbuf.shape[0]
     length = near + kbuf.shape[2]
     head_dim = width // heads
     block = 256
     tiles, near_tiles = length // 128, near // 128
+
+    def slot(r):
+        return lax.rem(r, slots)
 
     def tile_count(r):
         return (lens_ref[r, 0] + 127) // 128
@@ -276,7 +321,15 @@
             @pl.when(count == t)
             def _(size=(t - near_tiles) * 128):
                 body(lambda i: pltpu.make_async_copy(
-                    (ck_ref, cv_ref)[i].at[r, :, near:near + size], (kbuf, vbuf)[i].at[r, :, 0:size], in_sem.at[i, r]))
+                    (ck_ref, cv_ref)[i].at[r, :, near:near + size], (kbuf, vbuf)[i].at[slot(r), :, 0:size],
+                    in_sem.at[i, slot(r)]))
+
+    def far_start(r):
+        far_copies(r, lambda copy: (copy(0).start(), copy(1).start()))
+        for t in [t for t in range(1, tiles, 2) if t >= near_tiles]:
+            @pl.when(tile_count(r) == t)
+            def _(at=(t - near_tiles) * 128):
+                vbuf[slot(r), :, at:at + 128] = jnp.zeros((width, 128), BF16)
 
     def per_block(r, body):
         blocks = (lens_ref[r, 0] + block - 1) // block
@@ -285,24 +338,17 @@
             def _(size=t * block):
                 body(size)
 
-    @pl.loop(0, rows)
+    @pl.loop(0, slots)
     def _(r):
-        far_copies(r, lambda copy: (copy(0).start(), copy(1).start()))
+        far_start(r)
 
     spread_heads(q_ref, qblk, head_dim)
-
-    @pl.loop(0, rows)
-    def _(r):
-        for t in range(near_tiles + 1, tiles, 2):
-            @pl.when(tile_count(r) == t)
-            def _(at=(t - near_tiles) * 128):
-                vbuf[r, :, at:at + 128] = jnp.zeros((width, 128), BF16)
 
     def scores(r, size, out):
         first = min(size, near)
         out[:, 0:first] = dot_nn(qblk[r], kn_ref[r, :, 0:first])
         if size > near:
-            out[:, near:size] = dot_nn(qblk[r], kbuf[r, :, 0:size - near])
+            out[:, near:size] = dot_nn(qblk[r], kbuf[slot(r), :, 0:size - near])
 
     def softmax(r, src, out):
         keep = jnp.broadcast_to(mask_ref[pl.ds(r, 1), :], (HEAD_PAD, length)) == 1
@@ -312,7 +358,7 @@
         def tile(d, t):
             if t < near_tiles:
                 return vn_ref[r, d, t * 128:(t + 1) * 128]
-            return vbuf[r, d, (t - near_tiles) * 128:(t - near_tiles + 1) * 128]
+            return vbuf[slot(r), d, (t - near_tiles) * 128:(t - near_tiles + 1) * 128]
         cf[pl.ds(r, 1), :] = weighted_values(prob, tile, heads, head_dim, size)
 
     def arrived(r, i):
@@ -338,6 +384,10 @@
                 scores(r + 2, size_s, sa)
             per_block(r + 2, inner)
         per_block(r, outer)
+
+        @pl.when(r + slots < rows)
+        def _():
+            far_start(r + slots)
 
     @pl.loop(0, (rows - 2) // 2)
     def _(i):
@@ -354,41 +404,32 @@
     ctx_ref[...] = cf[...].astype(BF16)
 
 
-def ffn_kernel(n, ctx_ref, h1_ref, wo_hbm, ln_hbm, wr_hbm, idx_hbm, win_ref, wout_ref,
-               out_ref, cbuf, hpart, rbuf, ibuf, xbuf, mbuf, wi, wo, u0, u1, part, own, ybuf,
-               s1, r1, s2, r2, s3, r3, s4, r4, s5, r5, wi_sem, wo_sem,
-               wo_ref, ln_ref, wr_ref, idx_ref, in_sem):
+def ffn_kernel(n, ctx_ref, h1_ref, wo_ref, ln_hbm, rbuf, ibuf, early_ref, win_ref, wout_ref,
+               out_ref, cbuf, xbuf, mbuf, wi, wo, ubuf, part, own, ybuf,
+               s1, r1, s5, r5, wi_sem, wo_sem, ln_ref, in_sem):
     me = lax.axis_index("ws")
     rows, width = ctx_ref.shape
-    cols = wo_ref.shape[0]
     experts = win_ref.shape[0]
     total = n * rows
     capacity = (2 * total + experts - 1) // experts
 
+    early = early_ref.shape[0]
+
     def load(e, i):
-        src, buf, sem = ((win_ref, wi, wi_sem), (wout_ref, wo, wo_sem))[i]
-        return pltpu.make_async_copy(src.at[e], buf.at[e], sem.at[e])
-
-    loads = fetch([(idx_hbm, idx_ref), (wr_hbm, wr_ref), (wo_hbm, wo_ref), (ln_hbm, ln_ref)], in_sem)
-
-    @pl.loop(0, experts)
-    def _(e):
-        load(e, 0).start()
-        load(e, 1).start()
+        if i == 0:
+            return pltpu.make_async_copy(win_ref.at[e + early], wi.at[e], wi_sem.at[e])
+        return pltpu.make_async_copy(wout_ref.at[e], wo.at[e], wo_sem.at[e])
+
+    loads = fetch([(ln_hbm, ln_ref)], in_sem)
+
+    for i in range(2):
+        @pl.loop(0, experts - early if i == 0 else experts)
+        def _(e, i=i):
+            load(e, i).start()
 
     entry_barrier(me, n)
-    wait_all(loads)
-    first = (start_exchange(me, n, lambda p: ctx_ref, cbuf.at[me], s1, r1)
-             + start_exchange(me, n, lambda p: idx_ref, ibuf.at[me], s2, r2)
-             + start_exchange(me, n, lambda p: wr_ref, rbuf.at[me], s3, r3))
+    copies = start_exchange(me, n, lambda p: ctx_ref, cbuf.at[me], s1, r1)
     cbuf[me] = ctx_ref[...]
-    ibuf[me] = idx_ref[...]
-    rbuf[me] = wr_ref[...]
-    mine = my_columns(h1_ref[...].astype(F32), me, n, cols)
-    wait_all(first)
-    attn = dot_nt(cbuf[...].reshape(total, width), wo_ref[...])
-    hpart[me] = (mine + attn).astype(BF16)
-    copies = start_exchange(me, n, lambda p: hpart.at[me], hpart.at[me], s4, r4)
 
     idx_row = jnp.concatenate([ibuf[j] for j in range(n)], axis=1)
     grid_i = lax.broadcasted_iota(jnp.int32, (total, total), 0)
@@ -400,42 +441,47 @@
     target = jnp.where(slot < capacity, idx_col, -1)
     mbuf[...] = jnp.broadcast_to(target, mbuf.shape)
 
+    wait_all(loads)
     wait_all(copies)
-    h2 = jnp.concatenate([hpart[j] for j in range(n)], axis=1)
+    attn = dot_nt(cbuf[...].reshape(total, width), wo_ref[...].reshape(width, width))
+    h2 = (h1_ref[...].astype(F32) + attn).astype(BF16)
     x = rms_norm(h2, ln_ref[...].reshape(1, width))
     xbuf[...] = x
     own[...] = h2.reshape(n, rows, width)
-    def hidden_units(e, buf):
-        load(e, 0).wait()
-        u = jnp.maximum(dot_nn(xbuf[...], wi[e]), 0.0)
+    def hidden_units(e, weight):
+        u = jnp.maximum(dot_nn(xbuf[...], weight), 0.0)
         hit = jnp.broadcast_to(mbuf[:, 0:1], u.shape) == e
-        buf[...] = jnp.where(hit, u, 0.0).astype(BF16)
-
-    def add_output(e, buf):
-        part[...] += dot_nn(buf[...], wo[e]).reshape(part.shape)
-
-    part[...] = jnp.zeros_like(part)
-    hidden_units(0, u0)
-
-    @pl.loop(0, experts // 2)
+        ubuf[e] = jnp.where(hit, u, 0.0).astype(BF16)
+
+    @pl.loop(0, early // 2)
     def _(i):
-        e = i * 2
-        load(e, 1).wait()
-        hidden_units(e + 1, u1)
-        add_output(e, u0)
-        load(e + 1, 1).wait()
-
-        @pl.when(e + 2 < experts)
-        def _():
-            hidden_units(e + 2, u0)
-            add_output(e + 1, u1)
-
-        @pl.when(e + 2 >= experts)
-        def _():
-            add_output(e + 1, u1)
-
-    copies = start_exchange(me, n, lambda p: part.at[p], ybuf.at[me], s5, r5)
-    ybuf[me] = part[me]
+        for k in range(2):
+            hidden_units(i * 2 + k, early_ref[i * 2 + k])
+
+    @pl.loop(0, (experts - early) // 2)
+    def _(i):
+        for k in range(2):
+            load(i * 2 + k, 0).wait()
+        for k in range(2):
+            hidden_units(early + i * 2 + k, wi[i * 2 + k])
+
+    sends = []
+    block = part.shape[-1]
+    for c in range(width // block):
+        lanes = slice(c * block, (c + 1) * block)
+
+        def add_output(i, total, c=c, lanes=lanes):
+            if c == 0:
+                for k in range(4):
+                    load(i * 4 + k, 1).wait()
+            for k in range(4):
+                total = total + dot_nn(ubuf[i * 4 + k], wo[i * 4 + k, :, lanes])
+            return total
+        sums = lax.fori_loop(0, experts // 4, add_output, jnp.zeros((total, block), F32))
+        part[c] = sums.reshape(n, rows, block)
+        sends += start_exchange(me, n, lambda p: part.at[c, p], ybuf.at[c, me], s5.at[c], r5.at[c])
+        ybuf[c, me] = part[c, me]
+    copies = sends
 
     my_rows = pl.ds(pl.multiple_of(me * rows, rows), rows)
     router = jnp.concatenate([rbuf[j] for j in range(n)], axis=0)
@@ -446,9 +492,7 @@
     chosen = lax.broadcasted_iota(jnp.int32, (rows, experts), 1) == mbuf[my_rows, :][:, 0:experts]
     gate = jnp.sum(jnp.where(chosen, probs, 0.0), axis=-1, keepdims=True)
     wait_all(copies)
-    y = ybuf[0]
-    for j in range(1, n):
-        y = y + ybuf[j]
+    y = jnp.concatenate([sum(ybuf[c, j] for j in range(1, n)) + ybuf[c, 0] for c in range(width // block)], axis=1)
     out_ref[...] = (own[me].astype(F32) + y.astype(BF16).astype(F32) * gate).astype(BF16)
 
 
@@ -498,18 +542,19 @@
         sems = [dma((n - 1,))]
         w_tile = pltpu.VMEM((cols, width), BF16)
         ln_tile = pltpu.VMEM((width,), F32)
-        near = source // 2
-        q, k, v, hall, brev, lens, near_sk, near_sv = call(
+        near, slots, early = NEAR, SLOTS, EARLY
+        q, k, v, hall, brev, lens, wc_half, near_sk, near_sv = call(
             functools.partial(qkv_kernel, n),
-            [sds((rows, width), BF16)] * 3 + [sds((total, width), BF16), sds((HEAD_PAD, length), F32), sds((rows, 128), jnp.int32)]
+            [sds((rows, width), BF16)] * 3 + [sds((total, width), BF16), sds((HEAD_PAD, length), F32), sds((rows, 128), jnp.int32),
+               sds((cols // 2, width), BF16)]
             + [sds((rows, width, length), BF16)] * 2,
-            [HBM_SPEC] * 9, [VMEM_SPEC] * 8,
+            [HBM_SPEC] * 10, [VMEM_SPEC] * 9,
             [pltpu.VMEM((rows, width), BF16), ln_tile, pltpu.VMEM((3, cols, width), BF16), pltpu.VMEM((heads, length), F32),
              pltpu.VMEM((rows, source), jnp.int32),
              pltpu.VMEM((n, rows, width), BF16), pltpu.VMEM((n, 3, rows, cols), BF16), pltpu.VMEM((n, 3, rows, cols), BF16)]
-            + sems * 4 + [dma((7,)), dma((2, rows))],
+            + sems * 4 + [dma((8,)), dma((2, rows)), pltpu.VMEM((cols // 2, width), BF16), dma((2,)), dma((2,))],
             collective=0, vmem=8 << 20,
-        )(hidden, ln_self, wq_self.T, wk_self.T, wv_self.T, rel_bias, enc_mask, flat(self_k), flat(self_v))
+        )(hidden, ln_self, wq_self.T, wk_self.T, wv_self.T, rel_bias, enc_mask, wo_cross.T, flat(self_k), flat(self_v))
 
         def attention_scratch(size):
             return ([pltpu.VMEM((HEAD_PAD, size), F32)] * 4
@@ -525,38 +570,42 @@
             vmem=12 << 20,
         )(positions, q, k, v, brev, near_sk, near_sv)
 
-        qc, h1, near_ck, near_cv = call(
+        qc, h1, router, chosen, wc_full, near_ck, near_cv, early_w = call(
             functools.partial(mid_kernel, n),
-            [sds((rows, width), BF16), sds((total, width), BF16)] + [sds((rows, width, near), BF16)] * 2,
-            [VMEM_SPEC] * 2 + [HBM_SPEC] * 5, [VMEM_SPEC] * 4,
-            [w_tile, ln_tile, w_tile, dma((3,)), dma((2, rows)), pltpu.VMEM((n, rows, width), BF16), pltpu.VMEM((n, total, cols), BF16),
+            [sds((rows, width), BF16), sds((total, width), BF16), sds((n, experts // n, width), F32), sds((n, 1, rows), jnp.int32),
+               sds((n, cols, width), BF16)]
+            + [sds((rows, width, near), BF16)] * 2
+            + [sds((early, width, units), BF16)],
+            [VMEM_SPEC] * 2 + [HBM_SPEC] * 5 + [VMEM_SPEC] + [HBM_SPEC] * 4, [VMEM_SPEC] * 8,
+            [pltpu.VMEM((experts // n, width), F32), pltpu.VMEM((1, rows), jnp.int32)] + sems * 4
+            + [w_tile, dma((4,)), dma((4,)), w_tile, ln_tile, w_tile, dma((6,)), dma((2, rows)), dma((1, early)), pltpu.VMEM((n, rows, width), BF16), pltpu.VMEM((n, total, cols), BF16),
              pltpu.VMEM((n, rows, cols), BF16), pltpu.VMEM((n, rows, cols), BF16)] + sems * 6,
-            collective=1, vmem=8 << 20,
-        )(ctx, hall, wo_self.T, ln_cross, wq_cross.T, flat(cross_k), flat(cross_v))
+            collective=1, vmem=VM3 << 20,
+        )(ctx, hall, wo_self.T, ln_cross, wq_cross.T, w_router.T, expert_idx[None, :], wc_half, wo_cross.T, flat(cross_k), flat(cross_v), w_in)
 
         ctx2 = call(
             functools.partial(cross_kernel, heads),
             sds((rows, width), BF16),
             [SMEM_SPEC] + [VMEM_SPEC] * 4 + [HBM_SPEC] * 2, VMEM_SPEC,
-            [pltpu.VMEM((rows, width, source - near), BF16)] * 2 + attention_scratch(source) + [dma((2, rows))],
-            vmem=26 << 20,
+            [pltpu.VMEM((slots, width, source - near), BF16)] * 2 + attention_scratch(source) + [dma((2, slots))],
+            vmem=VM4 << 20,
         )(lens, qc, enc_mask, near_ck, near_cv, flat(cross_k), flat(cross_v))
 
+        parts = 3
         out = call(
             functools.partial(ffn_kernel, n),
             sds((rows, width), BF16),
-            [VMEM_SPEC] * 2 + [HBM_SPEC] * 6, VMEM_SPEC,
-            [pltpu.VMEM((n, rows, width), BF16), pltpu.VMEM((n, total, cols), BF16),
-             pltpu.VMEM((n, experts // n, width), F32), pltpu.VMEM((n, 1, rows), jnp.int32),
+            [VMEM_SPEC] * 3 + [HBM_SPEC] + [VMEM_SPEC] * 3 + [HBM_SPEC] * 2, VMEM_SPEC,
+            [pltpu.VMEM((n, rows, width), BF16),
              pltpu.VMEM((total, width), BF16), pltpu.VMEM((total, 128), jnp.int32),
-             pltpu.VMEM((experts, width, units), BF16), pltpu.VMEM((experts, units, width), BF16),
-             pltpu.VMEM((total, units), BF16), pltpu.VMEM((total, units), BF16),
-             pltpu.VMEM((n, rows, width), F32), pltpu.VMEM((n, rows, width), BF16),
-             pltpu.VMEM((n, rows, width), F32)]
-            + sems * 10 + [dma((experts,)), dma((experts,))]
-            + [w_tile, ln_tile, pltpu.VMEM((experts // n, width), F32), pltpu.VMEM((1, rows), jnp.int32), dma((4,))],
-            collective=2, vmem=41 << 20,
-        )(ctx2, h1, wo_cross.T, ln_ffn, w_router.T, expert_idx[None, :], w_in, w_out)
+             pltpu.VMEM((experts - early, width, units), BF16), pltpu.VMEM((experts, units, width), BF16),
+             pltpu.VMEM((experts, total, units), BF16),
+             pltpu.VMEM((parts, n, rows, width // parts), F32), pltpu.VMEM((n, rows, width), BF16),
+             pltpu.VMEM((parts, n, rows, width // parts), F32)]
+            + sems * 2 + [dma((parts, n - 1))] * 2 + [dma((experts,)), dma((experts,))]
+            + [ln_tile, dma((1,))],
+            collective=2, vmem=VM5 << 20,
+        )(ctx2, h1, wc_full, ln_ffn, router, chosen, early_w, w_in, w_out)
 
         def unflat(cache):
             return jnp.swapaxes(cache.reshape(rows, heads, head_dim, length), 2, 3)

time: 62.1 us -> 60.4 us (0.973)
  Pallas kernels: 60.7 us -> 59.2 us
    pallas_call x5, Pallas kernels: 60.7 us -> 59.2 us  [run(): kernel(*[pltpu.with_memory_space_constraint(x, pltpu.HBM) if spec is HBM_...]
where the time goes in v4:
time: 60.4 us; the launch traced here: 60.5 us
  Pallas kernels  59.2 us (98%)
  between operations  0.69 us (1%)
  local copies, waits for them, and re-layouts  0.62 us (1%)
    pallas_call x5, Pallas kernels, run(): kernel(*[pltpu.with_memory_space_constraint(x, pltpu.HBM) if spec is HBM_...  59.2 us

profile of v4, /device:TPU:0, one launch (start us, length us, event | category | flops | bytes accessed | tf_op | source)
XLA Modules:
  0.0 60.5 jit_solution(5305245080794763121)
XLA Ops:
  0.6 11.4 %shard_map.220 = (bf16[16,768]{1,0:T(8,128)(2,1)S(1)}, bf16[16,768]{1,0:T(8,128)(2,1)S(1)}, bf16[16,768]{1,0:T(8,128)(2,1)S(1)}, bf16[64,768]{1,0:T(8,128)(2,1)S...) custom-call(bf16[16,768]{1,0:T(8,128)(2,1)} %h_hbm.1, ...), custom_call_target="tpu_custom_call" | custom-call | flops 1000000 | bytes 1000000 | tf_op jit(solution)/shard_map/pallas_call | solution.py:509
  12.1 8.8 %shard_map.221 = (bf16[16,768]{1,0:T(8,128)(2,1)S(1)}, bf16[16,768,384]{2,1,0:T(8,128)(2,1)}, bf16[16,768,384]{2,1,0:T(8,128)(2,1)}) custom-call(s32[16]{0:T(128)} %pos_hbm.1, bf16[16,768]{1,0:T(8,128)(2,1)S(1)} %get-tuple-element.24.q_ref, bf16[16,768]{1,0:T(8,128)(2,1)S(1)} %get-tuple-element.25.k_ref, bf16[16,768]{1,0:T(8,128)(2,1)S(1)} %get-tuple-element.26.v_ref, ...), custom_call_target="tpu_custom_call" | custom-call | flops 1000000 | bytes 1000000 | tf_op jit(solution)/shard_map/pallas_call | solution.py:509
  20.9 0.0 copy-start
  20.9 12.5 %shard_map.222 = (bf16[16,768]{1,0:T(8,128)(2,1)S(1)}, bf16[64,768]{1,0:T(8,128)(2,1)S(1)}, f32[4,4,768]{2,1,0:T(4,128)S(1)}, s32[4,1,16]{2,1,0:T(1,128)S(1)}, b...) custom-call(bf16[16,768]{1,0:T(8,128)(2,1)S(1)} %get-tuple-element.3, ...), custom_call_target="tpu_custom_call" | custom-call | flops 1000000 | bytes 1000000 | tf_op jit(solution)/shard_map/pallas_call | solution.py:509
  33.4 0.0 copy-done
  33.5 9.5 %shard_map.223.ctx_ref = bf16[16,768]{1,0:T(8,128)(2,1)S(1)} custom-call(s32[16,128]{1,0:T(8,128)S(1)} %get-tuple-element.23.lens_ref, bf16[16,768]{1,0:T(8,128)(2,1)S(1)} %get-tuple-element.33.q_ref, s32[16,1024]{1,0:T(8,128)S(1)} %copy-done, bf16[16,768,512]{2,1,0:T(8,128)(2,1)S(1)} %get-tuple-element.34.kn_ref, ...), custom_call_target="tpu_custom_call" | custom-call | flops 1000000 | bytes 1000000 | tf_op jit(solution)/shard_map/pallas_call | solution.py:509
  42.9 16.9 %shard_map.224 = bf16[16,768]{1,0:T(8,128)(2,1)S(1)} custom-call(bf16[16,768]{1,0:T(8,128)(2,1)S(1)} %shard_map.223.ctx_ref, bf16[64,768]{1,0:T(8,128)(2,1)S(1)} %get-tuple-element.36.h1_ref, bf16[4,192,768]{2,1,0:T(8,128)(2,1)S(1)} %get-tuple-element.37.wo_ref, f32[768]{0:T(1024)} %ln_hbm.5, f32[4,4,768]{2,1,0:T(4,128)S(1)} %get-tuple-element.38.rbuf, ...), custom_call_target="tpu_custom_call" | custom-call | flops 1000000 | bytes 1000000 | tf_op jit(solution)/shard_map/pallas_call | solution.py:509
  59.9 0.6 %copy.25 = bf16[16,768]{1,0:T(8,128)(2,1)} copy(bf16[16,768]{1,0:T(8,128)(2,1)S(1)} %shard_map.224) | data formatting | bytes 49152
Async XLA Ops:
  20.9 12.6 %copy-start = (s32[16,1024]{1,0:T(8,128)S(1)}, s32[16,1024]{1,0:T(8,128)}, u32[]{:S(2)}) copy-start(s32[16,1024]{1,0:T(8,128)} %mask_ref.1) | copy-start | bytes 196612

commit v5 on v4

--- a/solution.py
+++ b/solution.py
@@ -119,8 +119,7 @@
     hbuf[me] = h_ref[...]
     other = {"ws": lax.rem(me + n // 2, n)}
     loads[1].wait()
-    cut = 80
-    bulk = [send(wc_own.at[0:cut], wc_half.at[0:cut], swc.at[0], rwc.at[0], other)]
+    bulk = [send(wc_own, wc_half, swc, rwc, other)]
     for load in loads[2:]:
         load.wait()
     lens_ref[...] = jnp.broadcast_to(jnp.sum(mask_ref[...], axis=1, keepdims=True), lens_ref.shape)
@@ -137,13 +136,12 @@
     for i in range(3):
         sendbuf[:, i] = dot_nt(x, w_ref[i]).astype(BF16).reshape(n, rows, cols)
     copies = start_exchange(me, n, lambda p: sendbuf.at[p], recvbuf.at[me], s2, r2)
-    bulk.append(send(wc_own.at[cut:half], wc_half.at[cut:half], swc.at[1], rwc.at[1], other))
     recvbuf[me] = sendbuf[me]
     wait_all(copies)
     for i, o in enumerate((q_ref, k_ref, v_ref)):
         o[...] = jnp.concatenate([recvbuf[j, i] for j in range(n)], axis=1)
+    wait_rows()
     wait_all(bulk)
-    wait_rows()
 
 
 def head_mask(shape, head_dim):
@@ -273,6 +271,8 @@
     cbuf[me] = ctx_ref[...]
     mine = my_columns(hall_ref[...].astype(F32), me, n, cols)
     wait_all(loads)
+    bulk += start_exchange(me, n, lambda p: wr_own, wr_ref.at[me], sr, rr)
+    bulk += start_exchange(me, n, lambda p: idx_own, idx_ref.at[me], si, ri)
     bulk.append(send(wc_own, wc_ref.at[me], sw.at[2], rw.at[2], {"ws": sibling}))
     wc_ref[me] = wc_own[...]
     wc_ref[facing, mine_half] = wc_half[...]
@@ -285,9 +285,7 @@
     h1_ref[...] = h1
     x = rms_norm(h1, ln_ref[...].reshape(1, width))
     sendbuf[...] = dot_nt(x, wq_ref[...]).astype(BF16).reshape(n, rows, cols)
-    copies = (start_exchange(me, n, lambda p: sendbuf.at[p], recvbuf.at[me], s3, r3)
-              + start_exchange(me, n, lambda p: wr_own, wr_ref.at[me], sr, rr)
-              + start_exchange(me, n, lambda p: idx_own, idx_ref.at[me], si, ri))
+    copies = start_exchange(me, n, lambda p: sendbuf.at[p], recvbuf.at[me], s3, r3)
     recvbuf[me] = sendbuf[me]
     wr_ref[me] = wr_own[...]
     idx_ref[me] = idx_own[...]
@@ -295,8 +293,8 @@
     bulk.append(send(wc_ref.at[facing, its_half], wc_ref.at[facing, its_half], sw.at[3], rw.at[3], {"ws": sibling}))
     wait_all(copies)
     q_ref[...] = jnp.concatenate([recvbuf[j] for j in range(n)], axis=1)
+    wait_rows()
     wait_all(bulk)
-    wait_rows()
     wait_win()
 
 
@@ -552,7 +550,7 @@
             [pltpu.VMEM((rows, width), BF16), ln_tile, pltpu.VMEM((3, cols, width), BF16), pltpu.VMEM((heads, length), F32),
              pltpu.VMEM((rows, source), jnp.int32),
              pltpu.VMEM((n, rows, width), BF16), pltpu.VMEM((n, 3, rows, cols), BF16), pltpu.VMEM((n, 3, rows, cols), BF16)]
-            + sems * 4 + [dma((8,)), dma((2, rows)), pltpu.VMEM((cols // 2, width), BF16), dma((2,)), dma((2,))],
+            + sems * 4 + [dma((8,)), dma((2, rows)), pltpu.VMEM((cols // 2, width), BF16), dma, dma],
             collective=0, vmem=8 << 20,
         )(hidden, ln_self, wq_self.T, wk_self.T, wv_self.T, rel_bias, enc_mask, wo_cross.T, flat(self_k), flat(self_v))
 

time: 60.4 us -> 59.5 us (0.985)
  Pallas kernels: 59.2 us -> 58.1 us
    pallas_call x5, Pallas kernels: 59.2 us -> 58.1 us  [run(): kernel(*[pltpu.with_memory_space_constraint(x, pltpu.HBM) if spec is HBM_...]
where the time goes in v5:
time: 59.5 us; the launch traced here: 59.4 us
  Pallas kernels  58.1 us (98%)
  between operations  0.69 us (1%)
  local copies, waits for them, and re-layouts  0.62 us (1%)
    pallas_call x5, Pallas kernels, run(): kernel(*[pltpu.with_memory_space_constraint(x, pltpu.HBM) if spec is HBM_...  58.1 us

profile of v5, /device:TPU:0, one launch (start us, length us, event | category | flops | bytes accessed | tf_op | source)
XLA Modules:
  0.0 59.4 jit_solution(13149674244751196555)
XLA Ops:
  0.6 10.7 %shard_map.220 = (bf16[16,768]{1,0:T(8,128)(2,1)S(1)}, bf16[16,768]{1,0:T(8,128)(2,1)S(1)}, bf16[16,768]{1,0:T(8,128)(2,1)S(1)}, bf16[64,768]{1,0:T(8,128)(2,1)S...) custom-call(bf16[16,768]{1,0:T(8,128)(2,1)} %h_hbm.1, ...), custom_call_target="tpu_custom_call" | custom-call | flops 1000000 | bytes 1000000 | tf_op jit(solution)/shard_map/pallas_call | solution.py:507
  11.4 8.8 %shard_map.221 = (bf16[16,768]{1,0:T(8,128)(2,1)S(1)}, bf16[16,768,384]{2,1,0:T(8,128)(2,1)}, bf16[16,768,384]{2,1,0:T(8,128)(2,1)}) custom-call(s32[16]{0:T(128)} %pos_hbm.1, bf16[16,768]{1,0:T(8,128)(2,1)S(1)} %get-tuple-element.24.q_ref, bf16[16,768]{1,0:T(8,128)(2,1)S(1)} %get-tuple-element.25.k_ref, bf16[16,768]{1,0:T(8,128)(2,1)S(1)} %get-tuple-element.26.v_ref, ...), custom_call_target="tpu_custom_call" | custom-call | flops 1000000 | bytes 1000000 | tf_op jit(solution)/shard_map/pallas_call | solution.py:507
  20.2 0.0 copy-start
  20.2 12.7 %shard_map.222 = (bf16[16,768]{1,0:T(8,128)(2,1)S(1)}, bf16[64,768]{1,0:T(8,128)(2,1)S(1)}, f32[4,4,768]{2,1,0:T(4,128)S(1)}, s32[4,1,16]{2,1,0:T(1,128)S(1)}, b...) custom-call(bf16[16,768]{1,0:T(8,128)(2,1)S(1)} %get-tuple-element.3, ...), custom_call_target="tpu_custom_call" | custom-call | flops 1000000 | bytes 1000000 | tf_op jit(solution)/shard_map/pallas_call | solution.py:507
  32.9 0.0 copy-done
  32.9 8.6 %shard_map.223.ctx_ref = bf16[16,768]{1,0:T(8,128)(2,1)S(1)} custom-call(s32[16,128]{1,0:T(8,128)S(1)} %get-tuple-element.23.lens_ref, bf16[16,768]{1,0:T(8,128)(2,1)S(1)} %get-tuple-element.33.q_ref, s32[16,1024]{1,0:T(8,128)S(1)} %copy-done, bf16[16,768,512]{2,1,0:T(8,128)(2,1)S(1)} %get-tuple-element.34.kn_ref, ...), custom_call_target="tpu_custom_call" | custom-call | flops 1000000 | bytes 1000000 | tf_op jit(solution)/shard_map/pallas_call | solution.py:507
  41.5 17.3 %shard_map.224 = bf16[16,768]{1,0:T(8,128)(2,1)S(1)} custom-call(bf16[16,768]{1,0:T(8,128)(2,1)S(1)} %shard_map.223.ctx_ref, bf16[64,768]{1,0:T(8,128)(2,1)S(1)} %get-tuple-element.36.h1_ref, bf16[4,192,768]{2,1,0:T(8,128)(2,1)S(1)} %get-tuple-element.37.wo_ref, f32[768]{0:T(1024)} %ln_hbm.5, f32[4,4,768]{2,1,0:T(4,128)S(1)} %get-tuple-element.38.rbuf, ...), custom_call_target="tpu_custom_call" | custom-call | flops 1000000 | bytes 1000000 | tf_op jit(solution)/shard_map/pallas_call | solution.py:507
  58.8 0.6 %copy.25 = bf16[16,768]{1,0:T(8,128)(2,1)} copy(bf16[16,768]{1,0:T(8,128)(2,1)S(1)} %shard_map.224) | data formatting | bytes 49152
Async XLA Ops:
  20.2 12.7 %copy-start = (s32[16,1024]{1,0:T(8,128)S(1)}, s32[16,1024]{1,0:T(8,128)}, u32[]{:S(2)}) copy-start(s32[16,1024]{1,0:T(8,128)} %mask_ref.1) | copy-start | bytes 196612

commit v6 on v5

--- a/solution.py
+++ b/solution.py
@@ -34,13 +34,16 @@
     return lax.dot_general(a, b, (((1,), (1,)), ((), ())), preferred_element_type=F32)
 
 
-def entry_barrier(me, n, across=None):
+def greet(me, n, across=None):
     sem = pltpu.get_barrier_semaphore()
     for k in range(1, n):
         pl.semaphore_signal(sem, inc=1, device_id={"ws": lax.rem(me + k, n)}, device_id_type=MESH)
     if across is not None:
         pl.semaphore_signal(sem, inc=1, device_id=across, device_id_type=MESH)
-    pl.semaphore_wait(sem, n - 1 if across is None else n)
+
+
+def all_here(count):
+    pl.semaphore_wait(pltpu.get_barrier_semaphore(), count)
 
 
 def send(src, dst, send_sem, recv_sem, device):
@@ -107,13 +110,14 @@
     me = lax.axis_index("ws")
     rows, width = h_ref.shape
     cols = w_ref.shape[1]
+    greet(me, n)
     half = cols // 2
     start = pl.multiple_of(lax.axis_index("dp") * half, 16)
     loads = fetch([(h_hbm, h_ref), (wc_hbm.at[pl.ds(start, half)], wc_own), (ln_hbm, ln_ref), (bias_hbm, bias_ref), (mask_hbm, mask_ref)]
                   + [(w, w_ref.at[i]) for i, w in enumerate((wq_hbm, wk_hbm, wv_hbm))], in_sem)
     start_rows, wait_rows = read_rows([(sk_hbm, sk_ref), (sv_hbm, sv_ref)], row_sem)
     start_rows()
-    entry_barrier(me, n)
+    all_here(n - 1)
     loads[0].wait()
     copies = start_exchange(me, n, lambda p: h_ref, hbuf.at[me], s1, r1)
     hbuf[me] = h_ref[...]
@@ -252,19 +256,20 @@
     me = lax.axis_index("ws")
     rows, width = ctx_ref.shape
     cols = wo_ref.shape[0]
+    group = lax.axis_index("dp")
+    across = {"dp": 1 - group, "ws": me}
+    greet(me, n, across)
     loads = fetch([(wo_hbm, wo_ref), (ln_hbm, ln_ref), (wq_hbm, wq_ref), (wr_hbm, wr_own), (idx_hbm, idx_own), (wc_hbm, wc_own)], in_sem)
     near = ck_ref.shape[2]
     start_rows, wait_rows = read_rows([(ck_hbm.at[:, :, 0:near], ck_ref), (cv_hbm.at[:, :, 0:near], cv_ref)], row_sem)
     start_win, wait_win = read_rows([(win_hbm, win_ref)], win_sem)
     start_rows()
     start_win()
-    group = lax.axis_index("dp")
     facing, sibling = lax.rem(me + n // 2, n), me + 1 - 2 * lax.rem(me, 2)
     half = cols // 2
     mine_half = pl.ds(pl.multiple_of(group * half, 16), half)
     its_half = pl.ds(pl.multiple_of((1 - group) * half, 16), half)
-    across = {"dp": 1 - group, "ws": me}
-    entry_barrier(me, n, across)
+    all_here(n)
     copies = start_exchange(me, n, lambda p: ctx_ref, cbuf.at[me], s1, r1)
     swap = send(wc_half, wc_ref.at[facing, mine_half], sw.at[0], rw.at[0], across)
     bulk = [send(wc_half, wc_ref.at[facing, mine_half], sw.at[1], rw.at[1], {"ws": sibling})]
@@ -418,6 +423,7 @@
             return pltpu.make_async_copy(win_ref.at[e + early], wi.at[e], wi_sem.at[e])
         return pltpu.make_async_copy(wout_ref.at[e], wo.at[e], wo_sem.at[e])
 
+    greet(me, n)
     loads = fetch([(ln_hbm, ln_ref)], in_sem)
 
     for i in range(2):
@@ -425,7 +431,7 @@
         def _(e, i=i):
             load(e, i).start()
 
-    entry_barrier(me, n)
+    all_here(n - 1)
     copies = start_exchange(me, n, lambda p: ctx_ref, cbuf.at[me], s1, r1)
     cbuf[me] = ctx_ref[...]
 

time: 59.5 us -> 59.3 us (level)
  no operation moved by 1% of the time
where the time goes in v6:
time: 59.3 us; the launch traced here: 59.1 us
  Pallas kernels  57.8 us (97%)
  between operations  0.69 us (1%)
  local copies, waits for them, and re-layouts  0.62 us (1%)
    pallas_call x5, Pallas kernels, run(): kernel(*[pltpu.with_memory_space_constraint(x, pltpu.HBM) if spec is HBM_...  57.8 us

profile of v6, /device:TPU:0, one launch (start us, length us, event | category | flops | bytes accessed | tf_op | source)
XLA Modules:
  0.0 59.1 jit_solution(14908318774514900780)
XLA Ops:
  0.6 10.6 %shard_map.220 = (bf16[16,768]{1,0:T(8,128)(2,1)S(1)}, bf16[16,768]{1,0:T(8,128)(2,1)S(1)}, bf16[16,768]{1,0:T(8,128)(2,1)S(1)}, bf16[64,768]{1,0:T(8,128)(2,1)S...) custom-call(bf16[16,768]{1,0:T(8,128)(2,1)} %h_hbm.1, ...), custom_call_target="tpu_custom_call" | custom-call | flops 1000000 | bytes 1000000 | tf_op jit(solution)/shard_map/pallas_call | solution.py:513
  11.2 8.8 %shard_map.221 = (bf16[16,768]{1,0:T(8,128)(2,1)S(1)}, bf16[16,768,384]{2,1,0:T(8,128)(2,1)}, bf16[16,768,384]{2,1,0:T(8,128)(2,1)}) custom-call(s32[16]{0:T(128)} %pos_hbm.1, bf16[16,768]{1,0:T(8,128)(2,1)S(1)} %get-tuple-element.24.q_ref, bf16[16,768]{1,0:T(8,128)(2,1)S(1)} %get-tuple-element.25.k_ref, bf16[16,768]{1,0:T(8,128)(2,1)S(1)} %get-tuple-element.26.v_ref, ...), custom_call_target="tpu_custom_call" | custom-call | flops 1000000 | bytes 1000000 | tf_op jit(solution)/shard_map/pallas_call | solution.py:513
  20.1 0.0 copy-start
  20.1 12.5 %shard_map.222 = (bf16[16,768]{1,0:T(8,128)(2,1)S(1)}, bf16[64,768]{1,0:T(8,128)(2,1)S(1)}, f32[4,4,768]{2,1,0:T(4,128)S(1)}, s32[4,1,16]{2,1,0:T(1,128)S(1)}, b...) custom-call(bf16[16,768]{1,0:T(8,128)(2,1)S(1)} %get-tuple-element.3, ...), custom_call_target="tpu_custom_call" | custom-call | flops 1000000 | bytes 1000000 | tf_op jit(solution)/shard_map/pallas_call | solution.py:513
  32.6 0.0 copy-done
  32.6 8.8 %shard_map.223.ctx_ref = bf16[16,768]{1,0:T(8,128)(2,1)S(1)} custom-call(s32[16,128]{1,0:T(8,128)S(1)} %get-tuple-element.23.lens_ref, bf16[16,768]{1,0:T(8,128)(2,1)S(1)} %get-tuple-element.33.q_ref, s32[16,1024]{1,0:T(8,128)S(1)} %copy-done, bf16[16,768,512]{2,1,0:T(8,128)(2,1)S(1)} %get-tuple-element.34.kn_ref, ...), custom_call_target="tpu_custom_call" | custom-call | flops 1000000 | bytes 1000000 | tf_op jit(solution)/shard_map/pallas_call | solution.py:513
  41.4 17.1 %shard_map.224 = bf16[16,768]{1,0:T(8,128)(2,1)S(1)} custom-call(bf16[16,768]{1,0:T(8,128)(2,1)S(1)} %shard_map.223.ctx_ref, bf16[64,768]{1,0:T(8,128)(2,1)S(1)} %get-tuple-element.36.h1_ref, bf16[4,192,768]{2,1,0:T(8,128)(2,1)S(1)} %get-tuple-element.37.wo_ref, f32[768]{0:T(1024)} %ln_hbm.5, f32[4,4,768]{2,1,0:T(4,128)S(1)} %get-tuple-element.38.rbuf, ...), custom_call_target="tpu_custom_call" | custom-call | flops 1000000 | bytes 1000000 | tf_op jit(solution)/shard_map/pallas_call | solution.py:513
  58.4 0.6 %copy.25 = bf16[16,768]{1,0:T(8,128)(2,1)} copy(bf16[16,768]{1,0:T(8,128)(2,1)S(1)} %shard_map.224) | data formatting | bytes 49152
Async XLA Ops:
  20.1 12.5 %copy-start = (s32[16,1024]{1,0:T(8,128)S(1)}, s32[16,1024]{1,0:T(8,128)}, u32[]{:S(2)}) copy-start(s32[16,1024]{1,0:T(8,128)} %mask_ref.1) | copy-start | bytes 196612

commit v7 on v6

--- a/solution.py
+++ b/solution.py
@@ -426,13 +426,17 @@
     greet(me, n)
     loads = fetch([(ln_hbm, ln_ref)], in_sem)
 
-    for i in range(2):
-        @pl.loop(0, experts - early if i == 0 else experts)
-        def _(e, i=i):
-            load(e, i).start()
+    @pl.loop(0, experts - early)
+    def _(e):
+        load(e, 0).start()
 
     all_here(n - 1)
     copies = start_exchange(me, n, lambda p: ctx_ref, cbuf.at[me], s1, r1)
+
+    @pl.loop(0, experts)
+    def _(e):
+        load(e, 1).start()
+
     cbuf[me] = ctx_ref[...]
 
     idx_row = jnp.concatenate([ibuf[j] for j in range(n)], axis=1)

time: 59.3 us -> 59.4 us (level)
  no operation moved by 1% of the time
where the time goes in v7:
time: 59.4 us; the launch traced here: 59.2 us
  Pallas kernels  57.9 us (97%)
  between operations  0.69 us (1%)
  local copies, waits for them, and re-layouts  0.62 us (1%)
    pallas_call x5, Pallas kernels, run(): kernel(*[pltpu.with_memory_space_constraint(x, pltpu.HBM) if spec is HBM_...  57.9 us

profile of v7, /device:TPU:0, one launch (start us, length us, event | category | flops | bytes accessed | tf_op | source)
XLA Modules:
  0.0 59.2 jit_solution(18312289914224065255)
XLA Ops:
  0.6 10.6 %shard_map.220 = (bf16[16,768]{1,0:T(8,128)(2,1)S(1)}, bf16[16,768]{1,0:T(8,128)(2,1)S(1)}, bf16[16,768]{1,0:T(8,128)(2,1)S(1)}, bf16[64,768]{1,0:T(8,128)(2,1)S...) custom-call(bf16[16,768]{1,0:T(8,128)(2,1)} %h_hbm.1, ...), custom_call_target="tpu_custom_call" | custom-call | flops 1000000 | bytes 1000000 | tf_op jit(solution)/shard_map/pallas_call | solution.py:517
  11.2 8.8 %shard_map.221 = (bf16[16,768]{1,0:T(8,128)(2,1)S(1)}, bf16[16,768,384]{2,1,0:T(8,128)(2,1)}, bf16[16,768,384]{2,1,0:T(8,128)(2,1)}) custom-call(s32[16]{0:T(128)} %pos_hbm.1, bf16[16,768]{1,0:T(8,128)(2,1)S(1)} %get-tuple-element.24.q_ref, bf16[16,768]{1,0:T(8,128)(2,1)S(1)} %get-tuple-element.25.k_ref, bf16[16,768]{1,0:T(8,128)(2,1)S(1)} %get-tuple-element.26.v_ref, ...), custom_call_target="tpu_custom_call" | custom-call | flops 1000000 | bytes 1000000 | tf_op jit(solution)/shard_map/pallas_call | solution.py:517
  20.1 0.0 copy-start
  20.1 12.5 %shard_map.222 = (bf16[16,768]{1,0:T(8,128)(2,1)S(1)}, bf16[64,768]{1,0:T(8,128)(2,1)S(1)}, f32[4,4,768]{2,1,0:T(4,128)S(1)}, s32[4,1,16]{2,1,0:T(1,128)S(1)}, b...) custom-call(bf16[16,768]{1,0:T(8,128)(2,1)S(1)} %get-tuple-element.3, ...), custom_call_target="tpu_custom_call" | custom-call | flops 1000000 | bytes 1000000 | tf_op jit(solution)/shard_map/pallas_call | solution.py:517
  32.6 0.0 copy-done
  32.6 8.2 %shard_map.223.ctx_ref = bf16[16,768]{1,0:T(8,128)(2,1)S(1)} custom-call(s32[16,128]{1,0:T(8,128)S(1)} %get-tuple-element.23.lens_ref, bf16[16,768]{1,0:T(8,128)(2,1)S(1)} %get-tuple-element.33.q_ref, s32[16,1024]{1,0:T(8,128)S(1)} %copy-done, bf16[16,768,512]{2,1,0:T(8,128)(2,1)S(1)} %get-tuple-element.34.kn_ref, ...), custom_call_target="tpu_custom_call" | custom-call | flops 1000000 | bytes 1000000 | tf_op jit(solution)/shard_map/pallas_call | solution.py:517
  40.8 17.9 %shard_map.224 = bf16[16,768]{1,0:T(8,128)(2,1)S(1)} custom-call(bf16[16,768]{1,0:T(8,128)(2,1)S(1)} %shard_map.223.ctx_ref, bf16[64,768]{1,0:T(8,128)(2,1)S(1)} %get-tuple-element.36.h1_ref, bf16[4,192,768]{2,1,0:T(8,128)(2,1)S(1)} %get-tuple-element.37.wo_ref, f32[768]{0:T(1024)} %ln_hbm.5, f32[4,4,768]{2,1,0:T(4,128)S(1)} %get-tuple-element.38.rbuf, ...), custom_call_target="tpu_custom_call" | custom-call | flops 1000000 | bytes 1000000 | tf_op jit(solution)/shard_map/pallas_call | solution.py:517
  58.6 0.6 %copy.25 = bf16[16,768]{1,0:T(8,128)(2,1)} copy(bf16[16,768]{1,0:T(8,128)(2,1)S(1)} %shard_map.224) | data formatting | bytes 49152
Async XLA Ops:
  20.1 12.5 %copy-start = (s32[16,1024]{1,0:T(8,128)S(1)}, s32[16,1024]{1,0:T(8,128)}, u32[]{:S(2)}) copy-start(s32[16,1024]{1,0:T(8,128)} %mask_ref.1) | copy-start | bytes 196612
